TPU v7x, 32 devices: a whole 2x2x4 slice. The times are simulated.
32 devices in a mesh: gx: 4 (over x, core), gy: 4 (over z), gz: 2 (over y).
Axes of the slice: x: 2, y: 2, z: 4, core: 2. Of those that a mesh axis runs over, the one named last changes fastest.
Arguments:
- orbitals: float32 [16, 32, 32, 512], P(None, 'gx', 'gy', 'gz'), may hold values from -10 to 10
- potential: float32 [32, 32, 512], P('gx', 'gy', 'gz'), may hold values from 0 to 12
Outputs:
- updated: float32 [16, 32, 32, 512], P(None, 'gx', 'gy', 'gz')
- trial_energies: float32 [16], replicated
All inputs are finite; a program needn't handle non-finite values.
Results may differ from a plain program's by a relative error of at most 0.000022.
Values sent between devices are 32-bit elements; how exact they have to be, the bound alone decides.
A program may use at most 64 MiB of HBM per device.

v0:
```python
import functools

import jax
import jax.numpy as jnp
from jax import lax
from jax.experimental import pallas as pl
from jax.experimental.pallas import tpu as pltpu
from jax.sharding import PartitionSpec as P

COARSE_SWEEPS = 4
WEIGHT = 0.8
COARSE_DIAG = 1.75
EPSILON = 1e-06
LANES = 128
ROWS = 8
GROUPS = 2
AXES = ("gx", "gy", "gz")
MESH = pl.DeviceIdType.MESH
NDOTS = 8


def kernel(sizes, orb_hbm, pot, out, energies, *scratch):
    (
        orb, app, res, cor, rsp, rem, coarse,
        fys, fyr, fzs, fzr, hy, cxs, cxr, cys, cyr, czs, czr, hcy,
        acc, scal, red, load_sem, send_sem, recv_sem, rsend, rrecv,
    ) = scratch
    nx, ny, nz = sizes
    bands, xs = orb_hbm.shape[0], orb_hbm.shape[1]
    tiles = orb_hbm.shape[3] // LANES
    xc = xs // 2
    per = bands // GROUPS
    me = [lax.axis_index(a) for a in AXES]
    right = [lax.rem(m + 1, n) for m, n in zip(me, sizes)]
    left = [lax.rem(m + n - 1, n) for m, n in zip(me, sizes)]

    loads = [
        pltpu.make_async_copy(
            orb_hbm.at[:, :, :, pl.ds(t * LANES, LANES)],
            orb.at[:, pl.ds(2, xs), t],
            load_sem.at[t],
        )
        for t in range(tiles)
    ]
    for c in loads:
        c.start()
    barrier = pltpu.get_barrier_semaphore()
    for k, a in enumerate(AXES):
        for d in range(1, sizes[k]):
            pl.semaphore_signal(
                barrier, inc=1, device_id={a: lax.rem(me[k] + d, sizes[k])}, device_id_type=MESH
            )
    pl.semaphore_wait(barrier, sum(sizes) - 3)
    for c in loads:
        c.wait()

    row = lax.broadcasted_iota(jnp.int32, (ROWS, LANES), 0)
    lane = lax.broadcasted_iota(jnp.int32, (ROWS, LANES), 1)
    even_lane = lane % 2 == 0
    even_row = row % 2 == 0
    low_half = lane < LANES // 2
    first_of_four = lane % 4 < 2

    def roll(v, k, axis):
        return pltpu.roll(v, k % v.shape[axis], axis)

    def flat(ref):
        n = 1
        for s in ref.shape[:-1]:
            n *= s
        return ref.reshape(n, LANES)

    def loop(lo, hi, f):
        def step(i, carry):
            f(i)
            return carry

        lax.fori_loop(lo, hi, step, 0)

    def remote(src, dst, slot, k, axis, target):
        return pltpu.make_async_remote_copy(
            src_ref=src,
            dst_ref=dst,
            send_sem=send_sem.at[slot, k],
            recv_sem=recv_sem.at[slot, k],
            device_id={axis: target},
            device_id_type=MESH,
        )

    def z_copies(src, dst_l, dst_r, slot):
        copies = [remote(src, dst_l, slot, 4, "gz", right[2])]
        if nz > 2:
            copies.append(remote(src, dst_r, slot, 5, "gz", left[2]))
        return copies

    def fine_send(field, which, depth, g):
        lo = g * per
        view = flat(field)
        span = field.shape[1]
        ys, yr = fys[which], fyr[which]
        zs, zr = fzs[which], fzr[which]

        def pack(b):
            for t in range(tiles):
                for j in range(depth):
                    base = ((b * span + 2) * tiles + t) * ROWS
                    ys[0, b, j, t] = view[pl.ds(base + ROWS - depth + j, xs, stride=tiles * ROWS), :]
                    ys[1, b, j, t] = view[pl.ds(base + j, xs, stride=tiles * ROWS), :]
            packed = jnp.zeros((ROWS, LANES), jnp.float32)
            for x in range(xs):
                w = jnp.where(low_half, field[b, 2 + x, 0], field[b, 2 + x, tiles - 1])
                packed = jnp.where(lane // 4 == x, roll(w, 2 + 4 * x, 1), packed)
            zs[b] = packed

        loop(lo, lo + per, pack)
        slot = which * GROUPS + g
        part = pl.ds(lo, per)
        copies = [
            remote(field.at[part, pl.ds(2 + xs - depth, depth)], field.at[part, pl.ds(2 - depth, depth)], slot, 0, "gx", right[0]),
            remote(field.at[part, pl.ds(2, depth)], field.at[part, pl.ds(2 + xs, depth)], slot, 1, "gx", left[0]),
            remote(ys.at[0, part], yr.at[0, part], slot, 2, "gy", right[1]),
            remote(ys.at[1, part], yr.at[1, part], slot, 3, "gy", left[1]),
        ] + z_copies(zs.at[part], zr.at[0, part], zr.at[1, part], slot)
        for c in copies:
            c.start()
        return copies

    def wait(copies):
        for c in copies:
            c.wait()

    def z_packed(zr, b):
        if nz > 2:
            return jnp.where(first_of_four, zr[0, b], zr[1, b])
        return zr[0, b]

    def unpack_y(yr, b, depth):
        view = flat(hy)
        for t in range(tiles):
            for j in range(depth):
                base = (b * xs * tiles + t) * ROWS
                view[pl.ds(base + ROWS - depth + j, xs, stride=tiles * ROWS), :] = yr(0, j, t)
                view[pl.ds(base + j, xs, stride=tiles * ROWS), :] = yr(1, j, t)

    def shifted_y(v, h, k):
        up = roll(jnp.where(row >= ROWS - k, h, v), k, 0)
        down = roll(jnp.where(row < k, h, v), -k, 0)
        return up + down

    def shifted_z(vs, hz, k):
        before = [hz] + vs[:-1]
        after = vs[1:] + [hz]
        return [
            roll(jnp.where(lane >= LANES - k, p, v), k, 1) + roll(jnp.where(lane < k, n, v), -k, 1)
            for p, v, n in zip(before, vs, after)
        ]

    def hamiltonian(field, which, b, use):
        unpack_y(lambda s, j, t: fyr[which][s, b, j, t], b, 2)
        zp = z_packed(fzr[which], b)
        for x in range(xs):
            hz = roll(zp, -(4 * x + 2), 1)
            vs = [field[b, 2 + x, t] for t in range(tiles)]
            z1, z2 = shifted_z(vs, hz, 1), shifted_z(vs, hz, 2)
            outs = []
            for t in range(tiles):
                h = hy[b, x, t]
                near = field[b, 1 + x, t] + field[b, 3 + x, t] + shifted_y(vs[t], h, 1) + z1[t]
                far = field[b, x, t] + field[b, 4 + x, t] + shifted_y(vs[t], h, 2) + z2[t]
                potential = pot[x, :, t * LANES : (t + 1) * LANES]
                outs.append((potential + 3.75) * vs[t] - (2.0 / 3.0) * near + (1.0 / 24.0) * far)
            use(x, vs, outs)

    def rowsum(vs):
        return jnp.sum(functools.reduce(jnp.add, vs), axis=0, keepdims=True)

    def reduce_all(index, ndots):
        wide = lax.broadcasted_iota(jnp.int32, (bands, LANES), 1)
        total = jnp.zeros((bands, LANES), jnp.float32)
        for q in range(ndots):
            total = jnp.where(wide == q, jnp.sum(acc[q], axis=1, keepdims=True), total)
        for stage, k in enumerate((2, 1, 0)):
            n = sizes[k]
            buf = red.at[index * 3 + stage]
            buf[me[k]] = total
            copies = []
            for d in range(1, n):
                copies.append(
                    pltpu.make_async_remote_copy(
                        src_ref=buf.at[me[k]],
                        dst_ref=buf.at[me[k]],
                        send_sem=rsend.at[index * 3 + stage, d],
                        recv_sem=rrecv.at[index * 3 + stage, d],
                        device_id={AXES[k]: lax.rem(me[k] + d, n)},
                        device_id_type=MESH,
                    )
                )
            for c in copies:
                c.start()
            for c in copies:
                c.wait()
            total = buf[0]
            for i in range(1, n):
                total = total + buf[i]
        return [total[:, q : q + 1] for q in range(ndots)]

    def put(k, column):
        scal[k] = jnp.broadcast_to(column, (bands, LANES))

    def get(k, b):
        return scal[k, pl.ds(b, 1), :]

    def restrict(b, ry, rz):
        unpack_y(ry, b, 1)
        for X in range(xc):
            pair = [None] * tiles
            for x in (2 * X, 2 * X + 1):
                hz = roll(rz, -(4 * x + 2), 1)
                vs = [res[b, 2 + x, t] for t in range(tiles)]
                z1 = shifted_z(vs, hz, 1)
                for t in range(tiles):
                    s = res[b, 1 + x, t] + res[b, 3 + x, t] + shifted_y(vs[t], hy[b, x, t], 1) + z1[t]
                    m = (1.0 - WEIGHT) * vs[t] + (0.5 * WEIGHT / 4.0) * s
                    rem[b, x, t] = m
                    pair[t] = m if pair[t] is None else pair[t] + m
            for t in range(tiles):
                s = pair[t]
                s = s + jnp.where(even_row, roll(s, -1, 0), roll(s, 1, 0))
                s = s + jnp.where(even_lane, roll(s, -1, 1), roll(s, 1, 1))
                coarse[0, b, 1 + X, t] = s * (0.125 * WEIGHT / COARSE_DIAG)

    def coarse_send(which, level, g):
        cf = coarse.at[level]
        view = flat(coarse)
        lo = g * per // 4

        def pack(i):
            b = 4 * i
            for t in range(tiles):
                for side, X in ((0, xc), (1, 1)):
                    lanes = [
                        jnp.where(even_lane, cf[b + k, X, t], cf[b + k + 1, X, t]) for k in (0, 2)
                    ]
                    cxs[which, side, i, t] = jnp.where(even_row, lanes[0], lanes[1])
                for side, j in ((0, ROWS - 1), (1, 0)):
                    vs = [
                        view[pl.ds((((level * bands + b + k) * (xc + 2) + 1) * tiles + t) * ROWS + j, xc, stride=tiles * ROWS), :]
                        for k in range(4)
                    ]
                    ev = even_lane[:xc]
                    cys[which, side, i, t, 0:xc] = jnp.where(ev, vs[0], vs[1])
                    cys[which, side, i, t, xc : 2 * xc] = jnp.where(ev, vs[2], vs[3])

        loop(lo, lo + per // 4, pack)

        def pack_z(i):
            packed = jnp.zeros((ROWS, LANES), jnp.float32)
            for k in range(8):
                for X in range(xc):
                    off = 4 * (k * xc + X)
                    w = jnp.where(low_half, cf[8 * i + k, 1 + X, 0], cf[8 * i + k, 1 + X, tiles - 1])
                    packed = jnp.where(lane // 4 == off // 4, roll(w, 2 + off, 1), packed)
            czs[which, i] = packed

        loop(g * per // 8, (g + 1) * per // 8, pack_z)
        slot = (4 + which) * GROUPS + g
        part = pl.ds(lo, per // 4)
        zpart = pl.ds(g * per // 8, per // 8)
        copies = [
            remote(cxs.at[which, 0, part], cxr.at[which, 0, part], slot, 0, "gx", right[0]),
            remote(cxs.at[which, 1, part], cxr.at[which, 1, part], slot, 1, "gx", left[0]),
            remote(cys.at[which, 0, part], cyr.at[which, 0, part], slot, 2, "gy", right[1]),
            remote(cys.at[which, 1, part], cyr.at[which, 1, part], slot, 3, "gy", left[1]),
        ] + z_copies(czs.at[which, zpart], czr.at[which, 0, zpart], czr.at[which, 1, zpart], slot)
        for c in copies:
            c.start()
        return copies

    def spread_lanes(p):
        return (
            jnp.where(even_lane, p, roll(p, 1, 1)),
            jnp.where(even_lane, roll(p, -1, 1), p),
        )

    def coarse_unpack(which, level, g):
        cf = coarse.at[level]
        view = flat(hcy)
        lo = g * per // 4

        def unpack(i):
            b = 4 * i
            for t in range(tiles):
                for side, X in ((0, 0), (1, xc + 1)):
                    p = cxr[which, side, i, t]
                    top = jnp.where(even_row, p, roll(p, 1, 0))
                    low = jnp.where(even_row, roll(p, -1, 0), p)
                    for k, v in enumerate(spread_lanes(top) + spread_lanes(low)):
                        cf[b + k, X, t] = v
                for side, j in ((0, ROWS - 2), (1, 0)):
                    first, second = spread_lanes(cyr[which, side, i, t])
                    for k, v in enumerate((first[:xc], second[:xc], first[xc:], second[xc:])):
                        base = ((b + k) * xc * tiles + t) * ROWS + j
                        for dup in range(2):
                            view[pl.ds(base + dup, xc, stride=tiles * ROWS), :] = v

        loop(lo, lo + per // 4, unpack)

    def coarse_loop(which, g, f):
        def bundle(i):
            zp = czr[which, 0, i]
            if nz > 2:
                zp = jnp.where(first_of_four, zp, czr[which, 1, i])
            for k in range(8):
                f(8 * i + k, lambda X, k=k: roll(zp, -(4 * (k * xc + X) + 2), 1))

        loop(g * per // 8, (g + 1) * per // 8, bundle)

    def sweep(which, level, g):
        coarse_unpack(which, level, g)

        def one(b, hz):
            for X in range(xc):
                vs = [coarse[level, b, 1 + X, t] for t in range(tiles)]
                z = shifted_z(vs, hz(X), 2)
                for t in range(tiles):
                    s = coarse[level, b, X, t] + coarse[level, b, 2 + X, t] + shifted_y(vs[t], hcy[b, X, t], 2) + z[t]
                    rhs = coarse[0, b, 1 + X, t]
                    coarse[level + 1, b, 1 + X, t] = (
                        (1.0 - WEIGHT) * vs[t] + (0.125 * WEIGHT / COARSE_DIAG) * s + rhs
                    )

        coarse_loop(which, g, one)

    def prolong(which, level, g, use):
        coarse_unpack(which, level, g)

        def one(b, hz):
            for X in range(xc):
                vs = [coarse[level, b, 1 + X, t] for t in range(tiles)]
                z = shifted_z(vs, hz(X), 1)
                for t in range(tiles):
                    s = shifted_y(vs[t], hcy[b, X, t], 1) + z[t] + vs[t]
                    for x, other in ((2 * X, X), (2 * X + 1, 2 + X)):
                        total = s + coarse[level, b, other, t]
                        kr = (1.0 - WEIGHT) * (res[b, 2 + x, t] + vs[t] + rem[b, x, t]) + (
                            0.5 * WEIGHT / 4.0
                        ) * total
                        use(b, x, t, kr)

        coarse_loop(which, g, one)

    groups = range(GROUPS)

    def precondition(base, prepare, use):
        flight = []
        for g in groups:
            loop(g * per, (g + 1) * per, prepare)
            flight.append(coarse_send(base, 0, g))
        for s in range(COARSE_SWEEPS - 1):
            for g in groups:
                wait(flight[g])
                sweep(base + s, s, g)
                flight[g] = coarse_send(base + s + 1, s + 1, g)
        for g in groups:
            wait(flight[g])
            prolong(base + COARSE_SWEEPS - 1, COARSE_SWEEPS - 1, g, use)
            yield g

    flight = [fine_send(orb, 0, 2, g) for g in groups]
    second = []
    for g in groups:
        wait(flight[g])

        def apply_one(b):
            norm, energy = [], []

            def use(x, vs, outs):
                for t in range(tiles):
                    app[b, 2 + x, t] = outs[t]
                    norm.append(vs[t] * vs[t])
                    energy.append(vs[t] * outs[t])

            hamiltonian(orb, 0, b, use)
            acc[0, pl.ds(b, 1), :] = rowsum(norm)
            acc[1, pl.ds(b, 1), :] = rowsum(energy)

        loop(g * per, (g + 1) * per, apply_one)
        second.append(fine_send(app, 1, 1, g))
    norm_orbitals, first_energy = reduce_all(0, 2)
    energy = first_energy / (norm_orbitals + EPSILON)
    put(0, energy)
    for c in second:
        wait(c)

    def prepare_first(b):
        e = get(0, b)
        for x in range(1, xs + 3):
            for t in range(tiles):
                res[b, x, t] = app[b, x, t] - e * orb[b, x, t]

        def ry(s, j, t):
            return fyr[1][s, b, 0, t] - e * fyr[0][s, b, 1 - s, t]

        restrict(b, ry, z_packed(fzr[1], b) - e * z_packed(fzr[0], b))

    def use_first(b, x, t, kr):
        cor[b, 2 + x, t] = kr

    flight = []
    for g in precondition(0, prepare_first, use_first):
        flight.append(fine_send(cor, 2, 2, g))
    second = []
    for g in groups:
        wait(flight[g])

        def respond_one(b):
            e = get(0, b)
            dots = [[] for _ in range(NDOTS)]

            def use(x, vs, outs):
                for t in range(tiles):
                    c, o, r = vs[t], orb[b, 2 + x, t], res[b, 2 + x, t]
                    p = outs[t] - e * c
                    rsp[b, 2 + x, t] = p
                    for q, (u, v) in enumerate(((r, p), (p, p), (o, c), (c, c), (p, o), (p, c), (r, o), (r, c))):
                        w = u * v
                        dots[q] = [w] if not dots[q] else [dots[q][0] + w]

            hamiltonian(cor, 2, b, use)
            for q in range(NDOTS):
                acc[q, pl.ds(b, 1), :] = rowsum(dots[q])

        loop(g * per, (g + 1) * per, respond_one)
        second.append(fine_send(rsp, 3, 1, g))
    rp, pp, oc, cc, po, pc, ro, rc = reduce_all(1, NDOTS)
    lam = -rp / (pp + EPSILON)
    trial_norm = norm_orbitals + 2.0 * lam * oc + lam * lam * cc
    trial_sum = (
        first_energy + lam * ((po + energy * oc) + (rc + energy * oc)) + lam * lam * (pc + energy * cc)
    )
    trial = trial_sum / (trial_norm + EPSILON)
    energies[...] = jnp.broadcast_to(trial, (bands, LANES))
    change = trial - energy
    projected = lam * rp - change * (ro + lam * rc)
    cross = po + lam * pc
    change_norm = lam * lam * pp - 2.0 * lam * change * cross + change * change * trial_norm
    mix = -projected / (change_norm + EPSILON)
    put(1, lam)
    put(2, mix * lam)
    put(3, mix * change)
    put(4, mix * change * lam)
    for c in second:
        wait(c)

    def prepare_second(b):
        e, ml, mc, mcl = get(0, b), get(2, b), get(3, b), get(4, b)

        def mixed(r, p, o, c):
            return r + ml * p - mc * o - mcl * c

        for x in range(1, xs + 3):
            for t in range(tiles):
                res[b, x, t] = mixed(res[b, x, t], rsp[b, x, t], orb[b, x, t], cor[b, x, t])

        def ry(s, j, t):
            o = fyr[0][s, b, 1 - s, t]
            r = fyr[1][s, b, 0, t] - e * o
            return mixed(r, fyr[3][s, b, 0, t], o, fyr[2][s, b, 1 - s, t])

        oz = z_packed(fzr[0], b)
        rz = z_packed(fzr[1], b) - e * oz
        restrict(b, ry, mixed(rz, z_packed(fzr[3], b), oz, z_packed(fzr[2], b)))

    def use_second(b, x, t, kr):
        out[b, x, :, t * LANES : (t + 1) * LANES] = (
            orb[b, 2 + x, t] + get(2, b) * cor[b, 2 + x, t] + get(1, b) * kr
        )

    for g in precondition(COARSE_SWEEPS, prepare_second, use_second):
        pass


def solution(mesh):
    sizes = tuple(mesh.shape[a] for a in AXES)

    def body(orbitals, potential):
        bands, xs, ys, zs = orbitals.shape
        tiles = zs // LANES
        tile = (ROWS, LANES)
        vmem = lambda *s: pltpu.VMEM(s + tile, jnp.float32)
        field = vmem(bands, xs + 4, tiles)
        exchanges = 4 + 2 * COARSE_SWEEPS
        faces = (2 * COARSE_SWEEPS, 2, bands // 4, tiles)
        peers = max(sizes)

        def call(*refs):
            refs = list(refs)
            head, rest = refs[:4], refs[4:]
            fields, rest = rest[:7], rest[7:]
            fys, rest = rest[:4], rest[4:]
            fyr, rest = rest[:4], rest[4:]
            fzs, rest = rest[:4], rest[4:]
            fzr, rest = rest[:4], rest[4:]
            kernel(sizes, *head, *fields, fys, fyr, fzs, fzr, *rest)

        depths = (2, 1, 2, 1)
        updated, trial = pl.pallas_call(
            call,
            out_shape=(
                jax.ShapeDtypeStruct(orbitals.shape, jnp.float32),
                jax.ShapeDtypeStruct((bands, LANES), jnp.float32),
            ),
            in_specs=[
                pl.BlockSpec(memory_space=pl.ANY),
                pl.BlockSpec(memory_space=pltpu.VMEM),
            ],
            out_specs=(
                pl.BlockSpec(memory_space=pltpu.VMEM),
                pl.BlockSpec(memory_space=pltpu.VMEM),
            ),
            scratch_shapes=[field] * 5
            + [vmem(bands, xs, tiles), vmem(COARSE_SWEEPS, bands, xs // 2 + 2, tiles)]
            + [vmem(2, bands, d, tiles) for d in depths]
            + [vmem(2, bands, d, tiles) for d in depths]
            + [vmem(bands) for d in depths]
            + [vmem(2, bands) for d in depths]
            + [
                vmem(bands, xs, tiles),
                vmem(*faces),
                vmem(*faces),
                vmem(*faces),
                vmem(*faces),
                vmem(2 * COARSE_SWEEPS, bands // 8),
                vmem(2 * COARSE_SWEEPS, 2, bands // 8),
                vmem(bands, xs // 2, tiles),
                pltpu.VMEM((NDOTS, bands, LANES), jnp.float32),
                pltpu.VMEM((5, bands, LANES), jnp.float32),
                pltpu.VMEM((6, peers, bands, LANES), jnp.float32),
                pltpu.SemaphoreType.DMA((tiles,)),
                pltpu.SemaphoreType.DMA((exchanges * GROUPS, 6)),
                pltpu.SemaphoreType.DMA((exchanges * GROUPS, 6)),
                pltpu.SemaphoreType.DMA((6, peers)),
                pltpu.SemaphoreType.DMA((6, peers)),
            ],
            compiler_params=pltpu.CompilerParams(
                collective_id=0, has_side_effects=True, vmem_limit_bytes=48 * 1024 * 1024
            ),
        )(orbitals, potential)
        return updated, trial[:, 0]

    return jax.shard_map(
        body,
        mesh=mesh,
        in_specs=(P(None, "gx", "gy", "gz"), P("gx", "gy", "gz")),
        out_specs=(P(None, "gx", "gy", "gz"), P()),
        check_vma=False,
    )
```

profile of v0, /device:TPU:0, one launch (start us, length us, event | category | flops | bytes accessed | tf_op | source)
XLA Modules:
  0.0 109.4 jit_solution(8578732818504427419)
XLA Ops:
  0.6 0.0 copy-start
  0.6 1.2 %copy-done = f32[16,8,8,256]{3,2,1,0:T(8,128)S(1)} copy-done((f32[16,8,8,256]{3,2,1,0:T(8,128)S(1)}, f32[16,8,8,256]{3,2,1,0:T(8,128)}, u32[]{:S(2)}) %copy-start) | copy-done | bytes 1048600
  1.9 0.0 copy-start.1
  1.9 0.8 copy-done.1
  2.7 105.1 %shard_map.41 = (f32[16,8,8,256]{3,2,1,0:T(8,128)S(1)}, f32[16,128]{1,0:T(8,128)S(1)}) custom-call(f32[16,8,8,256]{3,2,1,0:T(8,128)S(1)} %copy-done, f32[8,8,256]{2,1,0:T(8,128)S(1)} %copy-done.1), custom_call_target="tpu_custom_call" | custom-call | tf_op jit(solution)/shard_map/pallas_call | solution.py:507
  107.8 0.6 slice_reduce_fusion
  108.4 1.0 copy.5
Async XLA Ops:
  0.6 1.2 %copy-start = (f32[16,8,8,256]{3,2,1,0:T(8,128)S(1)}, f32[16,8,8,256]{3,2,1,0:T(8,128)}, u32[]{:S(2)}) copy-start(f32[16,8,8,256]{3,2,1,0:T(8,128)} %refs_0_.1) | copy-start | bytes 3145732
  1.9 0.8 copy-start.1
where the time goes:
time: 110 us; the launch traced here: 109 us
  Pallas kernels  105 us (95%)
  local copies, waits for them, and re-layouts  3.65 us (3%)
    pallas_call x1, Pallas kernels, body(): pl.pallas_call(call, out_shape=(jax.ShapeDtypeStruct(orbitals.shape, jnp....  105 us
    unnamed x5, local copies, waits for them, and re-layouts  3.03 us

commit v1 on v0

--- a/solution.py
+++ b/solution.py
@@ -17,6 +17,10 @@
 AXES = ("gx", "gy", "gz")
 MESH = pl.DeviceIdType.MESH
 NDOTS = 8
+
+PACK, APPLY, PREPARE, SWEEP = 0.35, 1.2, 1.1, 0.5
+FINE_LINK, COARSE_LINK = 1.4, 0.35
+HALO, PLANE, MIDDLE, START = 3.5, 2.0, 0.1, 2.0
 
 
 def kernel(sizes, orb_hbm, pot, out, energies, *scratch):
@@ -30,29 +34,34 @@
     tiles = orb_hbm.shape[3] // LANES
     xc = xs // 2
     per = bands // GROUPS
+    zper = min(per, 8)
     me = [lax.axis_index(a) for a in AXES]
     right = [lax.rem(m + 1, n) for m, n in zip(me, sizes)]
     left = [lax.rem(m + n - 1, n) for m, n in zip(me, sizes)]
 
     loads = [
-        pltpu.make_async_copy(
-            orb_hbm.at[:, :, :, pl.ds(t * LANES, LANES)],
-            orb.at[:, pl.ds(2, xs), t],
-            load_sem.at[t],
-        )
-        for t in range(tiles)
+        [
+            pltpu.make_async_copy(
+                orb_hbm.at[pl.ds(g * per, per), :, :, pl.ds(t * LANES, LANES)],
+                orb.at[pl.ds(g * per, per), pl.ds(2, xs), t],
+                load_sem.at[g, t],
+            )
+            for t in range(tiles)
+        ]
+        for g in range(GROUPS)
     ]
-    for c in loads:
-        c.start()
+    for group in loads:
+        for c in group:
+            c.start()
+
+    plane = [
+        {"gx": lax.rem(me[0] + d // nz, nx), "gz": lax.rem(me[2] + d % nz, nz)} for d in range(1, nx * nz)
+    ]
+    column = [{"gy": lax.rem(me[1] + d, ny)} for d in range(1, ny)]
     barrier = pltpu.get_barrier_semaphore()
-    for k, a in enumerate(AXES):
-        for d in range(1, sizes[k]):
-            pl.semaphore_signal(
-                barrier, inc=1, device_id={a: lax.rem(me[k] + d, sizes[k])}, device_id_type=MESH
-            )
-    pl.semaphore_wait(barrier, sum(sizes) - 3)
-    for c in loads:
-        c.wait()
+    for to in plane + column:
+        pl.semaphore_signal(barrier, inc=1, device_id=to, device_id_type=MESH)
+    energies[...] = jnp.zeros_like(energies)
 
     row = lax.broadcasted_iota(jnp.int32, (ROWS, LANES), 0)
     lane = lax.broadcasted_iota(jnp.int32, (ROWS, LANES), 1)
@@ -174,38 +183,52 @@
     def rowsum(vs):
         return jnp.sum(functools.reduce(jnp.add, vs), axis=0, keepdims=True)
 
-    def reduce_all(index, ndots):
-        wide = lax.broadcasted_iota(jnp.int32, (bands, LANES), 1)
-        total = jnp.zeros((bands, LANES), jnp.float32)
-        for q in range(ndots):
-            total = jnp.where(wide == q, jnp.sum(acc[q], axis=1, keepdims=True), total)
-        for stage, k in enumerate((2, 1, 0)):
-            n = sizes[k]
-            buf = red.at[index * 3 + stage]
-            buf[me[k]] = total
-            copies = []
-            for d in range(1, n):
-                copies.append(
-                    pltpu.make_async_remote_copy(
-                        src_ref=buf.at[me[k]],
-                        dst_ref=buf.at[me[k]],
-                        send_sem=rsend.at[index * 3 + stage, d],
-                        recv_sem=rrecv.at[index * 3 + stage, d],
-                        device_id={AXES[k]: lax.rem(me[k] + d, n)},
-                        device_id_type=MESH,
-                    )
-                )
-            for c in copies:
-                c.start()
-            for c in copies:
-                c.wait()
-            total = buf[0]
-            for i in range(1, n):
-                total = total + buf[i]
-        return [total[:, q : q + 1] for q in range(ndots)]
-
-    def put(k, column):
-        scal[k] = jnp.broadcast_to(column, (bands, LANES))
+    def reduce_send(k, stage, peers, here, value):
+        slot = here + stage * nx * nz
+        red[k, slot] = value
+        copies = [
+            pltpu.make_async_remote_copy(
+                src_ref=red.at[k, slot],
+                dst_ref=red.at[k, slot],
+                send_sem=rsend.at[k, stage * nx * nz + d],
+                recv_sem=rrecv.at[k, stage * nx * nz + d],
+                device_id=to,
+                device_id_type=MESH,
+            )
+            for d, to in enumerate(peers)
+        ]
+        for c in copies:
+            c.start()
+        return copies
+
+    def reduce_start(index, g, ndots):
+        total = jnp.zeros((ROWS, LANES), jnp.float32)
+        for i in range(ndots * per // ROWS):
+            part = jnp.sum(acc[index, g, i * ROWS : (i + 1) * ROWS, :], axis=1, keepdims=True)
+            total = jnp.where(lane == row + i * ROWS, part, total)
+        k = index * GROUPS + g
+        return reduce_send(k, 0, plane, me[0] * nz + me[2], jnp.sum(total, axis=0, keepdims=True))
+
+    def reduce_rows(k, first, count):
+        total = red[k, first]
+        for i in range(1, count):
+            total = total + red[k, first + i]
+        return total
+
+    def reduce_middle(index, g, copies):
+        k = index * GROUPS + g
+        wait(copies)
+        return reduce_send(k, 1, column, me[1], reduce_rows(k, 0, nx * nz))
+
+    def reduce_finish(index, g, ndots, copies):
+        k = index * GROUPS + g
+        wait(copies)
+        total = jnp.broadcast_to(reduce_rows(k, nx * nz, ny), (ROWS, LANES))
+        return [total if q == 0 else roll(total, -q * per, 1) for q in range(ndots)]
+
+    def put(k, g, values):
+        for b in range(per):
+            scal[k, g * per + b : g * per + b + 1, :] = jnp.broadcast_to(values[0:1, b : b + 1], (1, LANES))
 
     def get(k, b):
         return scal[k, pl.ds(b, 1), :]
@@ -255,17 +278,17 @@
 
         def pack_z(i):
             packed = jnp.zeros((ROWS, LANES), jnp.float32)
-            for k in range(8):
+            for k in range(zper):
                 for X in range(xc):
                     off = 4 * (k * xc + X)
-                    w = jnp.where(low_half, cf[8 * i + k, 1 + X, 0], cf[8 * i + k, 1 + X, tiles - 1])
+                    w = jnp.where(low_half, cf[zper * i + k, 1 + X, 0], cf[zper * i + k, 1 + X, tiles - 1])
                     packed = jnp.where(lane // 4 == off // 4, roll(w, 2 + off, 1), packed)
             czs[which, i] = packed
 
-        loop(g * per // 8, (g + 1) * per // 8, pack_z)
+        loop(g * per // zper, (g + 1) * per // zper, pack_z)
         slot = (4 + which) * GROUPS + g
         part = pl.ds(lo, per // 4)
-        zpart = pl.ds(g * per // 8, per // 8)
+        zpart = pl.ds(g * per // zper, per // zper)
         copies = [
             remote(cxs.at[which, 0, part], cxr.at[which, 0, part], slot, 0, "gx", right[0]),
             remote(cxs.at[which, 1, part], cxr.at[which, 1, part], slot, 1, "gx", left[0]),
@@ -310,10 +333,10 @@
             zp = czr[which, 0, i]
             if nz > 2:
                 zp = jnp.where(first_of_four, zp, czr[which, 1, i])
-            for k in range(8):
-                f(8 * i + k, lambda X, k=k: roll(zp, -(4 * (k * xc + X) + 2), 1))
-
-        loop(g * per // 8, (g + 1) * per // 8, bundle)
+            for k in range(zper):
+                f(zper * i + k, lambda X, k=k: roll(zp, -(4 * (k * xc + X) + 2), 1))
+
+        loop(g * per // zper, (g + 1) * per // zper, bundle)
 
     def sweep(which, level, g):
         coarse_unpack(which, level, g)
@@ -349,48 +372,18 @@
 
         coarse_loop(which, g, one)
 
-    groups = range(GROUPS)
-
-    def precondition(base, prepare, use):
-        flight = []
-        for g in groups:
-            loop(g * per, (g + 1) * per, prepare)
-            flight.append(coarse_send(base, 0, g))
-        for s in range(COARSE_SWEEPS - 1):
-            for g in groups:
-                wait(flight[g])
-                sweep(base + s, s, g)
-                flight[g] = coarse_send(base + s + 1, s + 1, g)
-        for g in groups:
-            wait(flight[g])
-            prolong(base + COARSE_SWEEPS - 1, COARSE_SWEEPS - 1, g, use)
-            yield g
-
-    flight = [fine_send(orb, 0, 2, g) for g in groups]
-    second = []
-    for g in groups:
-        wait(flight[g])
-
-        def apply_one(b):
-            norm, energy = [], []
-
-            def use(x, vs, outs):
-                for t in range(tiles):
-                    app[b, 2 + x, t] = outs[t]
-                    norm.append(vs[t] * vs[t])
-                    energy.append(vs[t] * outs[t])
-
-            hamiltonian(orb, 0, b, use)
-            acc[0, pl.ds(b, 1), :] = rowsum(norm)
-            acc[1, pl.ds(b, 1), :] = rowsum(energy)
-
-        loop(g * per, (g + 1) * per, apply_one)
-        second.append(fine_send(app, 1, 1, g))
-    norm_orbitals, first_energy = reduce_all(0, 2)
-    energy = first_energy / (norm_orbitals + EPSILON)
-    put(0, energy)
-    for c in second:
-        wait(c)
+    def apply_one(g, b):
+        norm, energy = [], []
+
+        def use(x, vs, outs):
+            for t in range(tiles):
+                app[b, 2 + x, t] = outs[t]
+                norm.append(vs[t] * vs[t])
+                energy.append(vs[t] * outs[t])
+
+        hamiltonian(orb, 0, b, use)
+        acc[0, g, pl.ds(b - g * per, 1), :] = rowsum(norm)
+        acc[0, g, pl.ds(b - g * per + per, 1), :] = rowsum(energy)
 
     def prepare_first(b):
         e = get(0, b)
@@ -406,51 +399,22 @@
     def use_first(b, x, t, kr):
         cor[b, 2 + x, t] = kr
 
-    flight = []
-    for g in precondition(0, prepare_first, use_first):
-        flight.append(fine_send(cor, 2, 2, g))
-    second = []
-    for g in groups:
-        wait(flight[g])
-
-        def respond_one(b):
-            e = get(0, b)
-            dots = [[] for _ in range(NDOTS)]
-
-            def use(x, vs, outs):
-                for t in range(tiles):
-                    c, o, r = vs[t], orb[b, 2 + x, t], res[b, 2 + x, t]
-                    p = outs[t] - e * c
-                    rsp[b, 2 + x, t] = p
-                    for q, (u, v) in enumerate(((r, p), (p, p), (o, c), (c, c), (p, o), (p, c), (r, o), (r, c))):
-                        w = u * v
-                        dots[q] = [w] if not dots[q] else [dots[q][0] + w]
-
-            hamiltonian(cor, 2, b, use)
-            for q in range(NDOTS):
-                acc[q, pl.ds(b, 1), :] = rowsum(dots[q])
-
-        loop(g * per, (g + 1) * per, respond_one)
-        second.append(fine_send(rsp, 3, 1, g))
-    rp, pp, oc, cc, po, pc, ro, rc = reduce_all(1, NDOTS)
-    lam = -rp / (pp + EPSILON)
-    trial_norm = norm_orbitals + 2.0 * lam * oc + lam * lam * cc
-    trial_sum = (
-        first_energy + lam * ((po + energy * oc) + (rc + energy * oc)) + lam * lam * (pc + energy * cc)
-    )
-    trial = trial_sum / (trial_norm + EPSILON)
-    energies[...] = jnp.broadcast_to(trial, (bands, LANES))
-    change = trial - energy
-    projected = lam * rp - change * (ro + lam * rc)
-    cross = po + lam * pc
-    change_norm = lam * lam * pp - 2.0 * lam * change * cross + change * change * trial_norm
-    mix = -projected / (change_norm + EPSILON)
-    put(1, lam)
-    put(2, mix * lam)
-    put(3, mix * change)
-    put(4, mix * change * lam)
-    for c in second:
-        wait(c)
+    def respond_one(g, b):
+        e = get(0, b)
+        dots = [None] * NDOTS
+
+        def use(x, vs, outs):
+            for t in range(tiles):
+                c, o, r = vs[t], orb[b, 2 + x, t], res[b, 2 + x, t]
+                p = outs[t] - e * c
+                rsp[b, 2 + x, t] = p
+                for q, (u, v) in enumerate(((r, p), (p, p), (o, c), (c, c), (p, o), (p, c), (r, o), (r, c))):
+                    w = u * v
+                    dots[q] = w if dots[q] is None else dots[q] + w
+
+        hamiltonian(cor, 2, b, use)
+        for q in range(NDOTS):
+            acc[1, g, pl.ds(b - g * per + q * per, 1), :] = rowsum([dots[q]])
 
     def prepare_second(b):
         e, ml, mc, mcl = get(0, b), get(2, b), get(3, b), get(4, b)
@@ -476,8 +440,80 @@
             orb[b, 2 + x, t] + get(2, b) * cor[b, 2 + x, t] + get(1, b) * kr
         )
 
-    for g in precondition(COARSE_SWEEPS, prepare_second, use_second):
-        pass
+    def precondition(base, g, prepare, use):
+        loop(g * per, (g + 1) * per, prepare)
+        flight = coarse_send(base, 0, g)
+        yield PREPARE, COARSE_LINK, HALO
+        for s in range(COARSE_SWEEPS - 1):
+            wait(flight)
+            sweep(base + s, s, g)
+            flight = coarse_send(base + s + 1, s + 1, g)
+            yield SWEEP, COARSE_LINK, HALO
+        wait(flight)
+        prolong(base + COARSE_SWEEPS - 1, COARSE_SWEEPS - 1, g, use)
+
+    def chain(g):
+        lo, hi = g * per, (g + 1) * per
+        wait(loads[g])
+        flight = fine_send(orb, 0, 2, g)
+        yield PACK, 2 * FINE_LINK, HALO
+        wait(flight)
+        loop(lo, hi, functools.partial(apply_one, g))
+        sums = reduce_start(0, g, 2)
+        flight = fine_send(app, 1, 1, g)
+        yield APPLY, FINE_LINK, PLANE
+        sums = reduce_middle(0, g, sums)
+        yield MIDDLE, 0.0, HALO
+        norm_orbitals, first_energy = reduce_finish(0, g, 2, sums)
+        energy = first_energy / (norm_orbitals + EPSILON)
+        put(0, g, energy)
+        wait(flight)
+        yield from precondition(0, g, prepare_first, use_first)
+        flight = fine_send(cor, 2, 2, g)
+        yield SWEEP + PACK, 2 * FINE_LINK, HALO
+        wait(flight)
+        loop(lo, hi, functools.partial(respond_one, g))
+        sums = reduce_start(1, g, NDOTS)
+        flight = fine_send(rsp, 3, 1, g)
+        yield APPLY, FINE_LINK, PLANE
+        sums = reduce_middle(1, g, sums)
+        yield MIDDLE, 0.0, HALO
+        rp, pp, oc, cc, po, pc, ro, rc = reduce_finish(1, g, NDOTS, sums)
+        lam = -rp / (pp + EPSILON)
+        trial_norm = norm_orbitals + 2.0 * lam * oc + lam * lam * cc
+        trial_sum = (
+            first_energy + lam * ((po + energy * oc) + (rc + energy * oc)) + lam * lam * (pc + energy * cc)
+        )
+        trial = trial_sum / (trial_norm + EPSILON)
+        mine = jnp.where(lane < per, trial, 0.0)
+        energies[...] = energies[...] + (mine if g == 0 else roll(mine, g * per, 1))
+        change = trial - energy
+        projected = lam * rp - change * (ro + lam * rc)
+        cross = po + lam * pc
+        change_norm = lam * lam * pp - 2.0 * lam * change * cross + change * change * trial_norm
+        mix = -projected / (change_norm + EPSILON)
+        put(1, g, lam)
+        put(2, g, mix * lam)
+        put(3, g, mix * change)
+        put(4, g, mix * change * lam)
+        wait(flight)
+        yield from precondition(COARSE_SWEEPS, g, prepare_second, use_second)
+        yield SWEEP, 0.0, 0.0
+
+    pl.semaphore_wait(barrier, len(plane) + len(column))
+    chains = [chain(g) for g in range(GROUPS)]
+    ready = [START * g for g in range(GROUPS)]
+    now = link = 0.0
+    while any(c is not None for c in chains):
+        g = min((g for g in range(GROUPS) if chains[g] is not None), key=lambda g: (ready[g], g))
+        step = next(chains[g], None)
+        if step is None:
+            chains[g] = None
+            continue
+        work, load, latency = step
+        now = max(now, ready[g]) + work
+        link = max(link, now) + load
+        ready[g] = link + latency
 
 
 def solution(mesh):
@@ -491,7 +527,9 @@
         field = vmem(bands, xs + 4, tiles)
         exchanges = 4 + 2 * COARSE_SWEEPS
         faces = (2 * COARSE_SWEEPS, 2, bands // 4, tiles)
-        peers = max(sizes)
+        slots = sizes[0] * sizes[2] + sizes[1]
+        per = bands // GROUPS
+        zbundles = bands // min(per, 8)
 
         def call(*refs):
             refs = list(refs)
@@ -508,7 +546,7 @@
             call,
             out_shape=(
                 jax.ShapeDtypeStruct(orbitals.shape, jnp.float32),
-                jax.ShapeDtypeStruct((bands, LANES), jnp.float32),
+                jax.ShapeDtypeStruct(tile, jnp.float32),
             ),
             in_specs=[
                 pl.BlockSpec(memory_space=pl.ANY),
@@ -530,23 +568,23 @@
                 vmem(*faces),
                 vmem(*faces),
                 vmem(*faces),
-                vmem(2 * COARSE_SWEEPS, bands // 8),
-                vmem(2 * COARSE_SWEEPS, 2, bands // 8),
+                vmem(2 * COARSE_SWEEPS, zbundles),
+                vmem(2 * COARSE_SWEEPS, 2, zbundles),
                 vmem(bands, xs // 2, tiles),
-                pltpu.VMEM((NDOTS, bands, LANES), jnp.float32),
+                pltpu.VMEM((2, GROUPS, NDOTS * per, LANES), jnp.float32),
                 pltpu.VMEM((5, bands, LANES), jnp.float32),
-                pltpu.VMEM((6, peers, bands, LANES), jnp.float32),
-                pltpu.SemaphoreType.DMA((tiles,)),
+                pltpu.VMEM((2 * GROUPS, slots, 1, LANES), jnp.float32),
+                pltpu.SemaphoreType.DMA((GROUPS, tiles)),
                 pltpu.SemaphoreType.DMA((exchanges * GROUPS, 6)),
                 pltpu.SemaphoreType.DMA((exchanges * GROUPS, 6)),
-                pltpu.SemaphoreType.DMA((6, peers)),
-                pltpu.SemaphoreType.DMA((6, peers)),
+                pltpu.SemaphoreType.DMA((2 * GROUPS, slots)),
+                pltpu.SemaphoreType.DMA((2 * GROUPS, slots)),
             ],
             compiler_params=pltpu.CompilerParams(
                 collective_id=0, has_side_effects=True, vmem_limit_bytes=48 * 1024 * 1024
             ),
         )(orbitals, potential)
-        return updated, trial[:, 0]
+        return updated, trial[0, :bands]
 
     return jax.shard_map(
         body,

time: 110 us -> 101 us (0.918)
  Pallas kernels: 105 us -> 97 us
    pallas_call x1, Pallas kernels: 105 us -> 97 us  [body(): pl.pallas_call(call, out_shape=(jax.ShapeDtypeStruct(orbitals.shape, jnp....]
where the time goes in v1:
time: 101 us
  Pallas kernels  97 us (96%)
  local copies, waits for them, and re-layouts  3.54 us (4%)
    pallas_call x1, Pallas kernels, body(): pl.pallas_call(call, out_shape=(jax.ShapeDtypeStruct(orbitals.shape, jnp....  97 us
    unnamed x5, local copies, waits for them, and re-layouts  3.03 us

profile of v1, /device:TPU:0, one launch (start us, length us, event | category | flops | bytes accessed | tf_op | source)
XLA Modules:
  0.0 101.2 jit_solution(15955955087567708985)
XLA Ops:
  0.6 0.0 copy-start
  0.6 1.2 %copy-done = f32[16,8,8,256]{3,2,1,0:T(8,128)S(1)} copy-done((f32[16,8,8,256]{3,2,1,0:T(8,128)S(1)}, f32[16,8,8,256]{3,2,1,0:T(8,128)}, u32[]{:S(2)}) %copy-start) | copy-done | bytes 1048600
  1.9 0.0 copy-start.1
  1.9 0.8 copy-done.1
  2.7 97.0 %shard_map.41 = (f32[16,8,8,256]{3,2,1,0:T(8,128)S(1)}, f32[8,128]{1,0:T(8,128)S(1)}) custom-call(f32[16,8,8,256]{3,2,1,0:T(8,128)S(1)} %copy-done, f32[8,8,256]{2,1,0:T(8,128)S(1)} %copy-done.1), custom_call_target="tpu_custom_call" | custom-call | tf_op jit(solution)/shard_map/pallas_call | solution.py:545
  99.7 0.5 slice_bitcast_fusion
  100.2 1.0 copy.5
Async XLA Ops:
  0.6 1.2 %copy-start = (f32[16,8,8,256]{3,2,1,0:T(8,128)S(1)}, f32[16,8,8,256]{3,2,1,0:T(8,128)}, u32[]{:S(2)}) copy-start(f32[16,8,8,256]{3,2,1,0:T(8,128)} %refs_0_.1) | copy-start | bytes 3145732
  1.9 0.8 copy-start.1

commit v2 on v1

--- a/solution.py
+++ b/solution.py
@@ -13,21 +13,17 @@
 EPSILON = 1e-06
 LANES = 128
 ROWS = 8
-GROUPS = 2
+GROUPS = 4
 AXES = ("gx", "gy", "gz")
 MESH = pl.DeviceIdType.MESH
 NDOTS = 8
 
-PACK, APPLY, PREPARE, SWEEP = 0.35, 1.2, 1.1, 0.5
-FINE_LINK, COARSE_LINK = 1.4, 0.35
-HALO, PLANE, MIDDLE, START = 3.5, 2.0, 0.1, 2.0
-
-
-def kernel(sizes, orb_hbm, pot, out, energies, *scratch):
+
+def kernel(sizes, orb_hbm, pot_hbm, out, energies, *scratch):
     (
         orb, app, res, cor, rsp, rem, coarse,
         fys, fyr, fzs, fzr, hy, cxs, cxr, cys, cyr, czs, czr, hcy,
-        acc, scal, red, load_sem, send_sem, recv_sem, rsend, rrecv,
+        acc, scal, keep, red, pot, load_sem, send_sem, recv_sem, rsend, rrecv,
     ) = scratch
     nx, ny, nz = sizes
     bands, xs = orb_hbm.shape[0], orb_hbm.shape[1]
@@ -35,33 +31,56 @@
     xc = xs // 2
     per = bands // GROUPS
     zper = min(per, 8)
+    devices = nx * ny * nz
     me = [lax.axis_index(a) for a in AXES]
     right = [lax.rem(m + 1, n) for m, n in zip(me, sizes)]
     left = [lax.rem(m + n - 1, n) for m, n in zip(me, sizes)]
 
-    loads = [
-        [
+    here = (me[0] * ny + me[1]) * nz + me[2]
+
+    def start(copies):
+        for c in copies:
+            c.start()
+
+    def wait(copies):
+        for c in copies:
+            c.wait()
+
+    pot_load = pltpu.make_async_copy(pot_hbm, pot, load_sem.at[GROUPS, 0])
+
+    def load_copies(g):
+        part = pl.ds(g * per, per)
+        return [
             pltpu.make_async_copy(
-                orb_hbm.at[pl.ds(g * per, per), :, :, pl.ds(t * LANES, LANES)],
-                orb.at[pl.ds(g * per, per), pl.ds(2, xs), t],
+                orb_hbm.at[part, :, :, pl.ds(t * LANES, LANES)],
+                orb.at[part, pl.ds(2, xs), t],
                 load_sem.at[g, t],
             )
             for t in range(tiles)
         ]
-        for g in range(GROUPS)
-    ]
-    for group in loads:
-        for c in group:
-            c.start()
-
-    plane = [
-        {"gx": lax.rem(me[0] + d // nz, nx), "gz": lax.rem(me[2] + d % nz, nz)} for d in range(1, nx * nz)
-    ]
-    column = [{"gy": lax.rem(me[1] + d, ny)} for d in range(1, ny)]
+
+    for g in range(GROUPS):
+        start(load_copies(g))
+    pot_load.start()
+
+    def wrap(k, d):
+        return lax.rem(me[k] + d, sizes[k])
+
+    def every_peer(f):
+        if devices <= 64:
+            xyz = [[me[k]] + [wrap(k, d) for d in range(1, sizes[k])] for k in range(3)]
+            for d in range(1, devices):
+                f((xyz[0][d // (ny * nz)], xyz[1][d // nz % ny], xyz[2][d % nz]))
+        else:
+
+            def step(d, carry):
+                f((wrap(0, d // (ny * nz)), wrap(1, lax.rem(d // nz, ny)), wrap(2, lax.rem(d, nz))))
+                return carry
+
+            lax.fori_loop(1, devices, step, 0)
+
     barrier = pltpu.get_barrier_semaphore()
-    for to in plane + column:
-        pl.semaphore_signal(barrier, inc=1, device_id=to, device_id_type=MESH)
-    energies[...] = jnp.zeros_like(energies)
+    every_peer(lambda to: pl.semaphore_signal(barrier, inc=1, device_id=to, device_id_type=MESH))
 
     row = lax.broadcasted_iota(jnp.int32, (ROWS, LANES), 0)
     lane = lax.broadcasted_iota(jnp.int32, (ROWS, LANES), 1)
@@ -102,12 +121,22 @@
             copies.append(remote(src, dst_r, slot, 5, "gz", left[2]))
         return copies
 
+    def fine_copies(field, which, depth, g):
+        slot = which * GROUPS + g
+        part = pl.ds(g * per, per)
+        ys, yr = fys[which], fyr[which]
+        zs, zr = fzs[which], fzr[which]
+        return [
+            remote(field.at[part, pl.ds(2 + xs - depth, depth)], field.at[part, pl.ds(2 - depth, depth)], slot, 0, "gx", right[0]),
+            remote(field.at[part, pl.ds(2, depth)], field.at[part, pl.ds(2 + xs, depth)], slot, 1, "gx", left[0]),
+            remote(ys.at[0, part], yr.at[0, part], slot, 2, "gy", right[1]),
+            remote(ys.at[1, part], yr.at[1, part], slot, 3, "gy", left[1]),
+        ] + z_copies(zs.at[part], zr.at[0, part], zr.at[1, part], slot)
+
     def fine_send(field, which, depth, g):
-        lo = g * per
         view = flat(field)
         span = field.shape[1]
-        ys, yr = fys[which], fyr[which]
-        zs, zr = fzs[which], fzr[which]
+        ys, zs = fys[which], fzs[which]
 
         def pack(b):
             for t in range(tiles):
@@ -121,22 +150,8 @@
                 packed = jnp.where(lane // 4 == x, roll(w, 2 + 4 * x, 1), packed)
             zs[b] = packed
 
-        loop(lo, lo + per, pack)
-        slot = which * GROUPS + g
-        part = pl.ds(lo, per)
-        copies = [
-            remote(field.at[part, pl.ds(2 + xs - depth, depth)], field.at[part, pl.ds(2 - depth, depth)], slot, 0, "gx", right[0]),
-            remote(field.at[part, pl.ds(2, depth)], field.at[part, pl.ds(2 + xs, depth)], slot, 1, "gx", left[0]),
-            remote(ys.at[0, part], yr.at[0, part], slot, 2, "gy", right[1]),
-            remote(ys.at[1, part], yr.at[1, part], slot, 3, "gy", left[1]),
-        ] + z_copies(zs.at[part], zr.at[0, part], zr.at[1, part], slot)
-        for c in copies:
-            c.start()
-        return copies
-
-    def wait(copies):
-        for c in copies:
-            c.wait()
+        loop(g * per, (g + 1) * per, pack)
+        start(fine_copies(field, which, depth, g))
 
     def z_packed(zr, b):
         if nz > 2:
@@ -183,52 +198,37 @@
     def rowsum(vs):
         return jnp.sum(functools.reduce(jnp.add, vs), axis=0, keepdims=True)
 
-    def reduce_send(k, stage, peers, here, value):
-        slot = here + stage * nx * nz
-        red[k, slot] = value
-        copies = [
-            pltpu.make_async_remote_copy(
-                src_ref=red.at[k, slot],
-                dst_ref=red.at[k, slot],
-                send_sem=rsend.at[k, stage * nx * nz + d],
-                recv_sem=rrecv.at[k, stage * nx * nz + d],
-                device_id=to,
-                device_id_type=MESH,
-            )
-            for d, to in enumerate(peers)
-        ]
-        for c in copies:
-            c.start()
-        return copies
-
     def reduce_start(index, g, ndots):
         total = jnp.zeros((ROWS, LANES), jnp.float32)
         for i in range(ndots * per // ROWS):
             part = jnp.sum(acc[index, g, i * ROWS : (i + 1) * ROWS, :], axis=1, keepdims=True)
             total = jnp.where(lane == row + i * ROWS, part, total)
         k = index * GROUPS + g
-        return reduce_send(k, 0, plane, me[0] * nz + me[2], jnp.sum(total, axis=0, keepdims=True))
-
-    def reduce_rows(k, first, count):
-        total = red[k, first]
-        for i in range(1, count):
-            total = total + red[k, first + i]
-        return total
-
-    def reduce_middle(index, g, copies):
+        red[k, here] = jnp.sum(total, axis=0, keepdims=True)
+
+        def send(to):
+            pltpu.make_async_remote_copy(
+                src_ref=red.at[k, here],
+                dst_ref=red.at[k, here],
+                send_sem=rsend.at[k],
+                recv_sem=rrecv.at[k],
+                device_id=to,
+                device_id_type=MESH,
+            ).start()
+
+        every_peer(send)
+
+    def reduce_finish(index, g, ndots):
         k = index * GROUPS + g
-        wait(copies)
-        return reduce_send(k, 1, column, me[1], reduce_rows(k, 0, nx * nz))
-
-    def reduce_finish(index, g, ndots, copies):
-        k = index * GROUPS + g
-        wait(copies)
-        total = jnp.broadcast_to(reduce_rows(k, nx * nz, ny), (ROWS, LANES))
+        rest = red.at[k, pl.ds(0, devices - 1)]
+        pltpu.make_async_copy(rest, rest, rrecv.at[k]).wait()
+        pltpu.make_async_copy(rest, rest, rsend.at[k]).wait()
+        total = jnp.broadcast_to(jnp.sum(red[k], axis=0), (ROWS, LANES))
         return [total if q == 0 else roll(total, -q * per, 1) for q in range(ndots)]
 
     def put(k, g, values):
         for b in range(per):
-            scal[k, g * per + b : g * per + b + 1, :] = jnp.broadcast_to(values[0:1, b : b + 1], (1, LANES))
+            scal[k, pl.ds(g * per + b, 1), :] = jnp.broadcast_to(values[0:1, b : b + 1], (1, LANES))
 
     def get(k, b):
         return scal[k, pl.ds(b, 1), :]
@@ -252,10 +252,21 @@
                 s = s + jnp.where(even_lane, roll(s, -1, 1), roll(s, 1, 1))
                 coarse[0, b, 1 + X, t] = s * (0.125 * WEIGHT / COARSE_DIAG)
 
+    def coarse_copies(which, g):
+        slot = (4 + which) * GROUPS + g
+        part = pl.ds(g * (per // 4), per // 4)
+        zpart = pl.ds(g * (per // zper), per // zper)
+        return [
+            remote(cxs.at[which, 0, part], cxr.at[which, 0, part], slot, 0, "gx", right[0]),
+            remote(cxs.at[which, 1, part], cxr.at[which, 1, part], slot, 1, "gx", left[0]),
+            remote(cys.at[which, 0, part], cyr.at[which, 0, part], slot, 2, "gy", right[1]),
+            remote(cys.at[which, 1, part], cyr.at[which, 1, part], slot, 3, "gy", left[1]),
+        ] + z_copies(czs.at[which, zpart], czr.at[which, 0, zpart], czr.at[which, 1, zpart], slot)
+
     def coarse_send(which, level, g):
         cf = coarse.at[level]
         view = flat(coarse)
-        lo = g * per // 4
+        lo = g * (per // 4)
 
         def pack(i):
             b = 4 * i
@@ -285,19 +296,8 @@
                     packed = jnp.where(lane // 4 == off // 4, roll(w, 2 + off, 1), packed)
             czs[which, i] = packed
 
-        loop(g * per // zper, (g + 1) * per // zper, pack_z)
-        slot = (4 + which) * GROUPS + g
-        part = pl.ds(lo, per // 4)
-        zpart = pl.ds(g * per // zper, per // zper)
-        copies = [
-            remote(cxs.at[which, 0, part], cxr.at[which, 0, part], slot, 0, "gx", right[0]),
-            remote(cxs.at[which, 1, part], cxr.at[which, 1, part], slot, 1, "gx", left[0]),
-            remote(cys.at[which, 0, part], cyr.at[which, 0, part], slot, 2, "gy", right[1]),
-            remote(cys.at[which, 1, part], cyr.at[which, 1, part], slot, 3, "gy", left[1]),
-        ] + z_copies(czs.at[which, zpart], czr.at[which, 0, zpart], czr.at[which, 1, zpart], slot)
-        for c in copies:
-            c.start()
-        return copies
+        loop(g * (per // zper), (g + 1) * (per // zper), pack_z)
+        start(coarse_copies(which, g))
 
     def spread_lanes(p):
         return (
@@ -308,7 +308,7 @@
     def coarse_unpack(which, level, g):
         cf = coarse.at[level]
         view = flat(hcy)
-        lo = g * per // 4
+        lo = g * (per // 4)
 
         def unpack(i):
             b = 4 * i
@@ -336,7 +336,7 @@
             for k in range(zper):
                 f(zper * i + k, lambda X, k=k: roll(zp, -(4 * (k * xc + X) + 2), 1))
 
-        loop(g * per // zper, (g + 1) * per // zper, bundle)
+        loop(g * (per // zper), (g + 1) * (per // zper), bundle)
 
     def sweep(which, level, g):
         coarse_unpack(which, level, g)
@@ -440,53 +440,56 @@
             orb[b, 2 + x, t] + get(2, b) * cor[b, 2 + x, t] + get(1, b) * kr
         )
 
-    def precondition(base, g, prepare, use):
-        loop(g * per, (g + 1) * per, prepare)
-        flight = coarse_send(base, 0, g)
-        yield PREPARE, COARSE_LINK, HALO
-        for s in range(COARSE_SWEEPS - 1):
-            wait(flight)
-            sweep(base + s, s, g)
-            flight = coarse_send(base + s + 1, s + 1, g)
-            yield SWEEP, COARSE_LINK, HALO
-        wait(flight)
-        prolong(base + COARSE_SWEEPS - 1, COARSE_SWEEPS - 1, g, use)
-
-    def chain(g):
-        lo, hi = g * per, (g + 1) * per
-        wait(loads[g])
-        flight = fine_send(orb, 0, 2, g)
-        yield PACK, 2 * FINE_LINK, HALO
-        wait(flight)
-        loop(lo, hi, functools.partial(apply_one, g))
-        sums = reduce_start(0, g, 2)
-        flight = fine_send(app, 1, 1, g)
-        yield APPLY, FINE_LINK, PLANE
-        sums = reduce_middle(0, g, sums)
-        yield MIDDLE, 0.0, HALO
-        norm_orbitals, first_energy = reduce_finish(0, g, 2, sums)
+    def coarse_solve(base, use, then):
+        for s in range(COARSE_SWEEPS):
+
+            def step(g, s=s):
+                wait(coarse_copies(base + s, g))
+                if s < COARSE_SWEEPS - 1:
+                    sweep(base + s, s, g)
+                    coarse_send(base + s + 1, s + 1, g)
+                else:
+                    prolong(base + s, s, g, use)
+                    then(g)
+
+            loop(0, GROUPS, step)
+
+    def begin(g):
+        wait(load_copies(g))
+        fine_send(orb, 0, 2, g)
+
+    def first_hamiltonian(g):
+        wait(fine_copies(orb, 0, 2, g))
+        loop(g * per, (g + 1) * per, functools.partial(apply_one, g))
+        reduce_start(0, g, 2)
+        fine_send(app, 1, 1, g)
+
+    def first_residual(g):
+        norm_orbitals, first_energy = reduce_finish(0, g, 2)
         energy = first_energy / (norm_orbitals + EPSILON)
+        for i, v in enumerate((norm_orbitals, first_energy, energy)):
+            keep[i, g] = v
         put(0, g, energy)
-        wait(flight)
-        yield from precondition(0, g, prepare_first, use_first)
-        flight = fine_send(cor, 2, 2, g)
-        yield SWEEP + PACK, 2 * FINE_LINK, HALO
-        wait(flight)
-        loop(lo, hi, functools.partial(respond_one, g))
-        sums = reduce_start(1, g, NDOTS)
-        flight = fine_send(rsp, 3, 1, g)
-        yield APPLY, FINE_LINK, PLANE
-        sums = reduce_middle(1, g, sums)
-        yield MIDDLE, 0.0, HALO
-        rp, pp, oc, cc, po, pc, ro, rc = reduce_finish(1, g, NDOTS, sums)
+        wait(fine_copies(app, 1, 1, g))
+        loop(g * per, (g + 1) * per, prepare_first)
+        coarse_send(0, 0, g)
+
+    def second_hamiltonian(g):
+        wait(fine_copies(cor, 2, 2, g))
+        loop(g * per, (g + 1) * per, functools.partial(respond_one, g))
+        reduce_start(1, g, NDOTS)
+        fine_send(rsp, 3, 1, g)
+
+    def second_residual(g):
+        norm_orbitals, first_energy, energy = (keep[i, g] for i in range(3))
+        rp, pp, oc, cc, po, pc, ro, rc = reduce_finish(1, g, NDOTS)
         lam = -rp / (pp + EPSILON)
         trial_norm = norm_orbitals + 2.0 * lam * oc + lam * lam * cc
         trial_sum = (
             first_energy + lam * ((po + energy * oc) + (rc + energy * oc)) + lam * lam * (pc + energy * cc)
         )
         trial = trial_sum / (trial_norm + EPSILON)
-        mine = jnp.where(lane < per, trial, 0.0)
-        energies[...] = energies[...] + (mine if g == 0 else roll(mine, g * per, 1))
+        energies[pl.ds(g, 1), :] = trial[0:1]
         change = trial - energy
         projected = lam * rp - change * (ro + lam * rc)
         cross = po + lam * pc
@@ -496,24 +499,19 @@
         put(2, g, mix * lam)
         put(3, g, mix * change)
         put(4, g, mix * change * lam)
-        wait(flight)
-        yield from precondition(COARSE_SWEEPS, g, prepare_second, use_second)
-        yield SWEEP, 0.0, 0.0
-
-    pl.semaphore_wait(barrier, len(plane) + len(column))
-    chains = [chain(g) for g in range(GROUPS)]
-    ready = [START * g for g in range(GROUPS)]
-    now = link = 0.0
-    while any(c is not None for c in chains):
-        g = min((g for g in range(GROUPS) if chains[g] is not None), key=lambda g: (ready[g], g))
-        step = next(chains[g], None)
-        if step is None:
-            chains[g] = None
-            continue
-        work, load, latency = step
-        now = max(now, ready[g]) + work
-        link = max(link, now) + load
-        ready[g] = link + latency
+        wait(fine_copies(rsp, 3, 1, g))
+        loop(g * per, (g + 1) * per, prepare_second)
+        coarse_send(COARSE_SWEEPS, 0, g)
+
+    pl.semaphore_wait(barrier, devices - 1)
+    loop(0, GROUPS, begin)
+    pot_load.wait()
+    loop(0, GROUPS, first_hamiltonian)
+    loop(0, GROUPS, first_residual)
+    coarse_solve(0, use_first, lambda g: fine_send(cor, 2, 2, g))
+    loop(0, GROUPS, second_hamiltonian)
+    loop(0, GROUPS, second_residual)
+    coarse_solve(COARSE_SWEEPS, use_second, lambda g: None)
 
 
 def solution(mesh):
@@ -527,7 +525,7 @@
         field = vmem(bands, xs + 4, tiles)
         exchanges = 4 + 2 * COARSE_SWEEPS
         faces = (2 * COARSE_SWEEPS, 2, bands // 4, tiles)
-        slots = sizes[0] * sizes[2] + sizes[1]
+        devices = sizes[0] * sizes[1] * sizes[2]
         per = bands // GROUPS
         zbundles = bands // min(per, 8)
 
@@ -549,8 +547,8 @@
                 jax.ShapeDtypeStruct(tile, jnp.float32),
             ),
             in_specs=[
-                pl.BlockSpec(memory_space=pl.ANY),
-                pl.BlockSpec(memory_space=pltpu.VMEM),
+                pl.BlockSpec(memory_space=pltpu.HBM),
+                pl.BlockSpec(memory_space=pltpu.HBM),
             ],
             out_specs=(
                 pl.BlockSpec(memory_space=pltpu.VMEM),
@@ -573,18 +571,20 @@
                 vmem(bands, xs // 2, tiles),
                 pltpu.VMEM((2, GROUPS, NDOTS * per, LANES), jnp.float32),
                 pltpu.VMEM((5, bands, LANES), jnp.float32),
-                pltpu.VMEM((2 * GROUPS, slots, 1, LANES), jnp.float32),
-                pltpu.SemaphoreType.DMA((GROUPS, tiles)),
+                vmem(3, GROUPS),
+                pltpu.VMEM((2 * GROUPS, devices, 1, LANES), jnp.float32),
+                pltpu.VMEM(potential.shape, jnp.float32),
+                pltpu.SemaphoreType.DMA((GROUPS + 1, tiles)),
                 pltpu.SemaphoreType.DMA((exchanges * GROUPS, 6)),
                 pltpu.SemaphoreType.DMA((exchanges * GROUPS, 6)),
-                pltpu.SemaphoreType.DMA((2 * GROUPS, slots)),
-                pltpu.SemaphoreType.DMA((2 * GROUPS, slots)),
+                pltpu.SemaphoreType.DMA((2 * GROUPS,)),
+                pltpu.SemaphoreType.DMA((2 * GROUPS,)),
             ],
             compiler_params=pltpu.CompilerParams(
                 collective_id=0, has_side_effects=True, vmem_limit_bytes=48 * 1024 * 1024
             ),
         )(orbitals, potential)
-        return updated, trial[0, :bands]
+        return updated, trial[:GROUPS, :per].reshape(bands)
 
     return jax.shard_map(
         body,

time: 101 us -> 89.5 us (0.89)
  Pallas kernels: 97 us -> 85.1 us
    pallas_call x1, Pallas kernels: 97 us -> 85.1 us  [body(): pl.pallas_call(call, out_shape=(jax.ShapeDtypeStruct(orbitals.shape, jnp....]
where the time goes in v2:
time: 89.5 us; the launch traced here: 89.3 us
  Pallas kernels  85.1 us (95%)
  local copies, waits for them, and re-layouts  3.62 us (4%)
    pallas_call x1, Pallas kernels, body(): pl.pallas_call(call, out_shape=(jax.ShapeDtypeStruct(orbitals.shape, jnp....  85.1 us
    unnamed x5, local copies, waits for them, and re-layouts  3.03 us

profile of v2, /device:TPU:0, one launch (start us, length us, event | category | flops | bytes accessed | tf_op | source)
XLA Modules:
  0.0 89.3 jit_solution(3241564391325940002)
XLA Ops:
  0.6 0.0 copy-start
  0.6 1.2 %copy-done = f32[16,8,8,256]{3,2,1,0:T(8,128)S(1)} copy-done((f32[16,8,8,256]{3,2,1,0:T(8,128)S(1)}, f32[16,8,8,256]{3,2,1,0:T(8,128)}, u32[]{:S(2)}) %copy-start) | copy-done | bytes 1048600
  1.9 0.0 copy-start.1
  1.9 0.8 copy-done.1
  2.7 85.1 %shard_map.41 = (f32[16,8,8,256]{3,2,1,0:T(8,128)S(1)}, f32[8,128]{1,0:T(8,128)S(1)}) custom-call(f32[16,8,8,256]{3,2,1,0:T(8,128)S(1)} %copy-done, f32[8,8,256]{2,1,0:T(8,128)S(1)} %copy-done.1), custom_call_target="tpu_custom_call" | custom-call | tf_op jit(solution)/shard_map/pallas_call | solution.py:543
  87.8 0.6 reshape.7
  88.4 1.0 %copy.5 = f32[16,8,8,256]{3,2,1,0:T(8,128)} copy(f32[16,8,8,256]{3,2,1,0:T(8,128)S(1)} %get-tuple-element.8) | data formatting | bytes 2097152
  (1 shorter events, 0.0 us)
Async XLA Ops:
  0.6 1.2 %copy-start = (f32[16,8,8,256]{3,2,1,0:T(8,128)S(1)}, f32[16,8,8,256]{3,2,1,0:T(8,128)}, u32[]{:S(2)}) copy-start(f32[16,8,8,256]{3,2,1,0:T(8,128)} %refs_0_.1) | copy-start | bytes 3145732
  1.9 0.8 copy-start.1

commit v3 on v2

--- a/solution.py
+++ b/solution.py
@@ -8,6 +8,7 @@
 from jax.sharding import PartitionSpec as P
 
 COARSE_SWEEPS = 4
+QUAD = 4
 WEIGHT = 0.8
 COARSE_DIAG = 1.75
 EPSILON = 1e-06
@@ -22,7 +23,7 @@
 def kernel(sizes, orb_hbm, pot_hbm, out, energies, *scratch):
     (
         orb, app, res, cor, rsp, rem, coarse,
-        fys, fyr, fzs, fzr, hy, cxs, cxr, cys, cyr, czs, czr, hcy,
+        fys, fyr, fzs, fzr, hy, beside, czs, czr, czm, dup, duph, dupz,
         acc, scal, keep, red, pot, load_sem, send_sem, recv_sem, rsend, rrecv,
     ) = scratch
     nx, ny, nz = sizes
@@ -30,7 +31,6 @@
     tiles = orb_hbm.shape[3] // LANES
     xc = xs // 2
     per = bands // GROUPS
-    zper = min(per, 8)
     devices = nx * ny * nz
     me = [lax.axis_index(a) for a in AXES]
     right = [lax.rem(m + 1, n) for m, n in zip(me, sizes)]
@@ -88,6 +88,8 @@
     even_row = row % 2 == 0
     low_half = lane < LANES // 2
     first_of_four = lane % 4 < 2
+    first_of_eight = lane % 8 < 4
+    top_half = row < ROWS // 2
 
     def roll(v, k, axis):
         return pltpu.roll(v, k % v.shape[axis], axis)
@@ -234,6 +236,7 @@
         return scal[k, pl.ds(b, 1), :]
 
     def restrict(b, ry, rz):
+        k = lax.rem(b, QUAD)
         unpack_y(ry, b, 1)
         for X in range(xc):
             pair = [None] * tiles
@@ -250,127 +253,141 @@
                 s = pair[t]
                 s = s + jnp.where(even_row, roll(s, -1, 0), roll(s, 1, 0))
                 s = s + jnp.where(even_lane, roll(s, -1, 1), roll(s, 1, 1))
-                coarse[0, b, 1 + X, t] = s * (0.125 * WEIGHT / COARSE_DIAG)
-
-    def coarse_copies(which, g):
-        slot = (4 + which) * GROUPS + g
-        part = pl.ds(g * (per // 4), per // 4)
-        zpart = pl.ds(g * (per // zper), per // zper)
+                dup[k, 1 + X, t] = s * (0.125 * WEIGHT / COARSE_DIAG)
+
+    def coarse_pack(level, g):
+        for X in range(xc):
+            for t in range(tiles):
+                lanes = [jnp.where(even_lane, dup[k, 1 + X, t], dup[k + 1, 1 + X, t]) for k in (0, 2)]
+                coarse[level, g, 2 + X, t] = jnp.where(even_row, lanes[0], lanes[1])
+
+    def coarse_copies(level, w, g):
+        slot = (4 + w) * GROUPS + g
+        own, side = coarse.at[level, g], beside.at[level, g]
+        low, high = pl.ds(0, ROWS // 2), pl.ds(ROWS // 2, ROWS // 2)
+        inner, last, first = pl.ds(2, xc), 1 + xc, 2
+        right_x, left_x = {"gx": right[0]}, {"gx": left[0]}
+        right_y, left_y = {"gy": right[1]}, {"gy": left[1]}
+        moves = [
+            (own.at[pl.ds(xc, 2)], own.at[pl.ds(0, 2)], right_x),
+            (own.at[pl.ds(2, 2)], own.at[pl.ds(2 + xc, 2)], left_x),
+            (own.at[inner, :, high], side.at[pl.ds(1, xc), :, high], right_y),
+            (own.at[inner, :, low], side.at[pl.ds(1, xc), :, low], left_y),
+            (own.at[last, :, high], side.at[0, :, high], right_x | right_y),
+            (own.at[last, :, low], side.at[0, :, low], right_x | left_y),
+            (own.at[first, :, high], side.at[1 + xc, :, high], left_x | right_y),
+            (own.at[first, :, low], side.at[1 + xc, :, low], left_x | left_y),
+        ]
+        for end, z in enumerate((right[2], left[2])[: 1 if nz == 2 else 2]):
+            for i, to in enumerate(({}, right_x, left_x, right_y, left_y)):
+                moves.append((czs.at[w, g], czr.at[w, i, end, g], to | {"gz": z}))
         return [
-            remote(cxs.at[which, 0, part], cxr.at[which, 0, part], slot, 0, "gx", right[0]),
-            remote(cxs.at[which, 1, part], cxr.at[which, 1, part], slot, 1, "gx", left[0]),
-            remote(cys.at[which, 0, part], cyr.at[which, 0, part], slot, 2, "gy", right[1]),
-            remote(cys.at[which, 1, part], cyr.at[which, 1, part], slot, 3, "gy", left[1]),
-        ] + z_copies(czs.at[which, zpart], czr.at[which, 0, zpart], czr.at[which, 1, zpart], slot)
-
-    def coarse_send(which, level, g):
-        cf = coarse.at[level]
-        view = flat(coarse)
-        lo = g * (per // 4)
-
-        def pack(i):
-            b = 4 * i
-            for t in range(tiles):
-                for side, X in ((0, xc), (1, 1)):
-                    lanes = [
-                        jnp.where(even_lane, cf[b + k, X, t], cf[b + k + 1, X, t]) for k in (0, 2)
-                    ]
-                    cxs[which, side, i, t] = jnp.where(even_row, lanes[0], lanes[1])
-                for side, j in ((0, ROWS - 1), (1, 0)):
-                    vs = [
-                        view[pl.ds((((level * bands + b + k) * (xc + 2) + 1) * tiles + t) * ROWS + j, xc, stride=tiles * ROWS), :]
-                        for k in range(4)
-                    ]
-                    ev = even_lane[:xc]
-                    cys[which, side, i, t, 0:xc] = jnp.where(ev, vs[0], vs[1])
-                    cys[which, side, i, t, xc : 2 * xc] = jnp.where(ev, vs[2], vs[3])
-
-        loop(lo, lo + per // 4, pack)
-
-        def pack_z(i):
-            packed = jnp.zeros((ROWS, LANES), jnp.float32)
-            for k in range(zper):
-                for X in range(xc):
-                    off = 4 * (k * xc + X)
-                    w = jnp.where(low_half, cf[zper * i + k, 1 + X, 0], cf[zper * i + k, 1 + X, tiles - 1])
-                    packed = jnp.where(lane // 4 == off // 4, roll(w, 2 + off, 1), packed)
-            czs[which, i] = packed
-
-        loop(g * (per // zper), (g + 1) * (per // zper), pack_z)
-        start(coarse_copies(which, g))
-
-    def spread_lanes(p):
-        return (
-            jnp.where(even_lane, p, roll(p, 1, 1)),
-            jnp.where(even_lane, roll(p, -1, 1), p),
+            pltpu.make_async_remote_copy(
+                src_ref=src,
+                dst_ref=dst,
+                send_sem=send_sem.at[slot, k],
+                recv_sem=recv_sem.at[slot, k],
+                device_id=to,
+                device_id_type=MESH,
+            )
+            for k, (src, dst, to) in enumerate(moves)
+        ]
+
+    def coarse_send(level, w, g):
+        packed = jnp.zeros((ROWS, LANES), jnp.float32)
+        for X in range(xc):
+            v = jnp.where(low_half, coarse[level, g, 2 + X, 0], coarse[level, g, 2 + X, tiles - 1])
+            packed = jnp.where(lane // 8 == X, roll(v, 8 * X + 4, 1), packed)
+        czs[w, g] = packed
+        start(coarse_copies(level, w, g))
+
+    def z_edges(w, i, g):
+        if nz > 2:
+            return jnp.where(first_of_eight, czr[w, i, 0, g], czr[w, i, 1, g])
+        return czr[w, i, 0, g]
+
+    def z_halo(packed, X):
+        return roll(packed, -(8 * X + 4), 1)
+
+    def update(v, s, rhs):
+        return (1.0 - WEIGHT) * v + (0.125 * WEIGHT / COARSE_DIAG) * s + rhs
+
+    def sweep_plane(zero, level, g, X, hz):
+        vs = [coarse[level, g, 2 + X, t] for t in range(tiles)]
+        z = shifted_z(vs, hz, 2)
+        for t in range(tiles):
+            s = coarse[level, g, 1 + X, t] + coarse[level, g, 3 + X, t]
+            s = s + shifted_y(vs[t], beside[level, g, 1 + X, t], 2) + z[t]
+            coarse[level + 1, g, 2 + X, t] = update(vs[t], s, coarse[zero, g, 2 + X, t])
+
+    def sweep_wide(zero, level, w, g):
+        zc, from_left, from_right, from_below, from_above = (z_edges(w, i, g) for i in range(5))
+        zs, zy = czs[w, g], jnp.where(top_half, from_above, from_below)
+        for X in range(-1, xc + 1):
+            if X < 0:
+                hz = z_halo(from_left, xc - 1)
+            elif X == xc:
+                hz = z_halo(from_right, 0)
+            else:
+                hz = z_halo(zc, X)
+            sweep_plane(zero, level, g, X, hz)
+        for X in range(xc):
+            hs = [beside[level, g, 1 + X, t] for t in range(tiles)]
+            z = shifted_z(hs, z_halo(zy, X), 2)
+            for t in range(tiles):
+                h, v = hs[t], coarse[level, g, 2 + X, t]
+                y = jnp.where(top_half, roll(h, -2, 0) + roll(v, 2, 0), roll(h, 2, 0) + roll(v, -2, 0))
+                s = beside[level, g, X, t] + beside[level, g, 2 + X, t] + y + z[t]
+                beside[level + 1, g, 1 + X, t] = update(h, s, beside[zero, g, 1 + X, t])
+        edge = 8 * (xc - 1)
+        s = jnp.where(lane < 8, roll(from_left, -edge, 1), roll(zc, 8, 1))
+        s = s + jnp.where(lane >= edge, roll(from_right, edge, 1), roll(zc, -8, 1))
+        s = s + shifted_y(zc, zy, 2)
+        s = s + jnp.where(
+            first_of_eight, roll(zc, 2, 1) + roll(zs, -2, 1), roll(zc, -2, 1) + roll(zs, 2, 1)
         )
-
-    def coarse_unpack(which, level, g):
-        cf = coarse.at[level]
-        view = flat(hcy)
-        lo = g * (per // 4)
-
-        def unpack(i):
-            b = 4 * i
-            for t in range(tiles):
-                for side, X in ((0, 0), (1, xc + 1)):
-                    p = cxr[which, side, i, t]
-                    top = jnp.where(even_row, p, roll(p, 1, 0))
-                    low = jnp.where(even_row, roll(p, -1, 0), p)
-                    for k, v in enumerate(spread_lanes(top) + spread_lanes(low)):
-                        cf[b + k, X, t] = v
-                for side, j in ((0, ROWS - 2), (1, 0)):
-                    first, second = spread_lanes(cyr[which, side, i, t])
-                    for k, v in enumerate((first[:xc], second[:xc], first[xc:], second[xc:])):
-                        base = ((b + k) * xc * tiles + t) * ROWS + j
-                        for dup in range(2):
-                            view[pl.ds(base + dup, xc, stride=tiles * ROWS), :] = v
-
-        loop(lo, lo + per // 4, unpack)
-
-    def coarse_loop(which, g, f):
-        def bundle(i):
-            zp = czr[which, 0, i]
-            if nz > 2:
-                zp = jnp.where(first_of_four, zp, czr[which, 1, i])
-            for k in range(zper):
-                f(zper * i + k, lambda X, k=k: roll(zp, -(4 * (k * xc + X) + 2), 1))
-
-        loop(g * (per // zper), (g + 1) * (per // zper), bundle)
-
-    def sweep(which, level, g):
-        coarse_unpack(which, level, g)
-
-        def one(b, hz):
+        czm[w, g] = update(zc, s, z_edges(w // 2 * 2, 0, g))
+
+    def sweep_own(zero, level, w, g):
+        zc = czm[w, g]
+        for X in range(xc):
+            sweep_plane(zero, level, g, X, z_halo(zc, X))
+
+    def spread(p):
+        out = []
+        for v in (jnp.where(even_row, p, roll(p, 1, 0)), jnp.where(even_row, roll(p, -1, 0), p)):
+            out.append(jnp.where(even_lane, v, roll(v, 1, 1)))
+            out.append(jnp.where(even_lane, roll(v, -1, 1), v))
+        return out
+
+    def prolong(level, w, g, use):
+        zc = czm[w, g]
+        for X in range(xc + 2):
+            for t in range(tiles):
+                for k, v in enumerate(spread(coarse[level, g, 1 + X, t])):
+                    dup[k, X, t] = v
+        for X in range(xc):
+            for t in range(tiles):
+                for k, v in enumerate(spread(beside[level, g, 1 + X, t])):
+                    duph[k, X, t] = v
+            for k, v in enumerate(spread(z_halo(zc, X))):
+                dupz[k, X] = v
+
+        def one(b):
+            k = lax.rem(b, QUAD)
             for X in range(xc):
-                vs = [coarse[level, b, 1 + X, t] for t in range(tiles)]
-                z = shifted_z(vs, hz(X), 2)
+                vs = [dup[k, 1 + X, t] for t in range(tiles)]
+                z = shifted_z(vs, dupz[k, X], 1)
                 for t in range(tiles):
-                    s = coarse[level, b, X, t] + coarse[level, b, 2 + X, t] + shifted_y(vs[t], hcy[b, X, t], 2) + z[t]
-                    rhs = coarse[0, b, 1 + X, t]
-                    coarse[level + 1, b, 1 + X, t] = (
-                        (1.0 - WEIGHT) * vs[t] + (0.125 * WEIGHT / COARSE_DIAG) * s + rhs
-                    )
-
-        coarse_loop(which, g, one)
-
-    def prolong(which, level, g, use):
-        coarse_unpack(which, level, g)
-
-        def one(b, hz):
-            for X in range(xc):
-                vs = [coarse[level, b, 1 + X, t] for t in range(tiles)]
-                z = shifted_z(vs, hz(X), 1)
-                for t in range(tiles):
-                    s = shifted_y(vs[t], hcy[b, X, t], 1) + z[t] + vs[t]
+                    s = shifted_y(vs[t], duph[k, X, t], 1) + z[t] + vs[t]
                     for x, other in ((2 * X, X), (2 * X + 1, 2 + X)):
-                        total = s + coarse[level, b, other, t]
+                        total = s + dup[k, other, t]
                         kr = (1.0 - WEIGHT) * (res[b, 2 + x, t] + vs[t] + rem[b, x, t]) + (
                             0.5 * WEIGHT / 4.0
                         ) * total
                         use(b, x, t, kr)
 
-        coarse_loop(which, g, one)
+        loop(g * per, (g + 1) * per, one)
 
     def apply_one(g, b):
         norm, energy = [], []
@@ -440,19 +457,28 @@
             orb[b, 2 + x, t] + get(2, b) * cor[b, 2 + x, t] + get(1, b) * kr
         )
 
-    def coarse_solve(base, use, then):
-        for s in range(COARSE_SWEEPS):
-
-            def step(g, s=s):
-                wait(coarse_copies(base + s, g))
-                if s < COARSE_SWEEPS - 1:
-                    sweep(base + s, s, g)
-                    coarse_send(base + s + 1, s + 1, g)
-                else:
-                    prolong(base + s, s, g, use)
-                    then(g)
-
-            loop(0, GROUPS, step)
+    def coarse_begin(turn, g):
+        coarse_pack(turn * COARSE_SWEEPS, g)
+        coarse_send(turn * COARSE_SWEEPS, 2 * turn, g)
+
+    def coarse_solve(turn, use, then):
+        zero = turn * COARSE_SWEEPS
+        w = 2 * turn
+
+        def middle(g):
+            wait(coarse_copies(zero, w, g))
+            sweep_wide(zero, zero, w, g)
+            sweep_own(zero, zero + 1, w, g)
+            coarse_send(zero + 2, w + 1, g)
+
+        def finish(g):
+            wait(coarse_copies(zero + 2, w + 1, g))
+            sweep_wide(zero, zero + 2, w + 1, g)
+            prolong(zero + 3, w + 1, g, use)
+            then(g)
+
+        loop(0, GROUPS, middle)
+        loop(0, GROUPS, finish)
 
     def begin(g):
         wait(load_copies(g))
@@ -472,7 +498,7 @@
         put(0, g, energy)
         wait(fine_copies(app, 1, 1, g))
         loop(g * per, (g + 1) * per, prepare_first)
-        coarse_send(0, 0, g)
+        coarse_begin(0, g)
 
     def second_hamiltonian(g):
         wait(fine_copies(cor, 2, 2, g))
@@ -501,7 +527,7 @@
         put(4, g, mix * change * lam)
         wait(fine_copies(rsp, 3, 1, g))
         loop(g * per, (g + 1) * per, prepare_second)
-        coarse_send(COARSE_SWEEPS, 0, g)
+        coarse_begin(1, g)
 
     pl.semaphore_wait(barrier, devices - 1)
     loop(0, GROUPS, begin)
@@ -511,7 +537,7 @@
     coarse_solve(0, use_first, lambda g: fine_send(cor, 2, 2, g))
     loop(0, GROUPS, second_hamiltonian)
     loop(0, GROUPS, second_residual)
-    coarse_solve(COARSE_SWEEPS, use_second, lambda g: None)
+    coarse_solve(1, use_second, lambda g: None)
 
 
 def solution(mesh):
@@ -523,11 +549,10 @@
         tile = (ROWS, LANES)
         vmem = lambda *s: pltpu.VMEM(s + tile, jnp.float32)
         field = vmem(bands, xs + 4, tiles)
-        exchanges = 4 + 2 * COARSE_SWEEPS
-        faces = (2 * COARSE_SWEEPS, 2, bands // 4, tiles)
+        exchanges = 8
+        assert bands == QUAD * GROUPS
         devices = sizes[0] * sizes[1] * sizes[2]
         per = bands // GROUPS
-        zbundles = bands // min(per, 8)
 
         def call(*refs):
             refs = list(refs)
@@ -555,28 +580,28 @@
                 pl.BlockSpec(memory_space=pltpu.VMEM),
             ),
             scratch_shapes=[field] * 5
-            + [vmem(bands, xs, tiles), vmem(COARSE_SWEEPS, bands, xs // 2 + 2, tiles)]
+            + [vmem(bands, xs, tiles), vmem(2 * COARSE_SWEEPS, GROUPS, xs // 2 + 4, tiles)]
             + [vmem(2, bands, d, tiles) for d in depths]
             + [vmem(2, bands, d, tiles) for d in depths]
             + [vmem(bands) for d in depths]
             + [vmem(2, bands) for d in depths]
             + [
                 vmem(bands, xs, tiles),
-                vmem(*faces),
-                vmem(*faces),
-                vmem(*faces),
-                vmem(*faces),
-                vmem(2 * COARSE_SWEEPS, zbundles),
-                vmem(2 * COARSE_SWEEPS, 2, zbundles),
-                vmem(bands, xs // 2, tiles),
+                vmem(2 * COARSE_SWEEPS, GROUPS, xs // 2 + 2, tiles),
+                vmem(4, GROUPS),
+                vmem(4, 5, 2, GROUPS),
+                vmem(4, GROUPS),
+                vmem(QUAD, xs // 2 + 2, tiles),
+                vmem(QUAD, xs // 2, tiles),
+                vmem(QUAD, xs // 2),
                 pltpu.VMEM((2, GROUPS, NDOTS * per, LANES), jnp.float32),
                 pltpu.VMEM((5, bands, LANES), jnp.float32),
                 vmem(3, GROUPS),
                 pltpu.VMEM((2 * GROUPS, devices, 1, LANES), jnp.float32),
                 pltpu.VMEM(potential.shape, jnp.float32),
                 pltpu.SemaphoreType.DMA((GROUPS + 1, tiles)),
-                pltpu.SemaphoreType.DMA((exchanges * GROUPS, 6)),
-                pltpu.SemaphoreType.DMA((exchanges * GROUPS, 6)),
+                pltpu.SemaphoreType.DMA((exchanges * GROUPS, 18)),
+                pltpu.SemaphoreType.DMA((exchanges * GROUPS, 18)),
                 pltpu.SemaphoreType.DMA((2 * GROUPS,)),
                 pltpu.SemaphoreType.DMA((2 * GROUPS,)),
             ],

time: 89.5 us -> 84.4 us (0.943)
  Pallas kernels: 85.1 us -> 79.9 us
    pallas_call x1, Pallas kernels: 85.1 us -> 79.9 us  [body(): pl.pallas_call(call, out_shape=(jax.ShapeDtypeStruct(orbitals.shape, jnp....]
where the time goes in v3:
time: 84.4 us; the launch traced here: 84.2 us
  Pallas kernels  79.9 us (95%)
  local copies, waits for them, and re-layouts  3.62 us (4%)
    pallas_call x1, Pallas kernels, body(): pl.pallas_call(call, out_shape=(jax.ShapeDtypeStruct(orbitals.shape, jnp....  79.9 us
    unnamed x5, local copies, waits for them, and re-layouts  3.03 us

profile of v3, /device:TPU:0, one launch (start us, length us, event | category | flops | bytes accessed | tf_op | source)
XLA Modules:
  0.0 84.2 jit_solution(1520190906829225888)
XLA Ops:
  0.6 0.0 copy-start
  0.6 1.2 %copy-done = f32[16,8,8,256]{3,2,1,0:T(8,128)S(1)} copy-done((f32[16,8,8,256]{3,2,1,0:T(8,128)S(1)}, f32[16,8,8,256]{3,2,1,0:T(8,128)}, u32[]{:S(2)}) %copy-start) | copy-done | bytes 1048600
  1.9 0.0 copy-start.1
  1.9 0.8 copy-done.1
  2.7 79.9 %shard_map.41 = (f32[16,8,8,256]{3,2,1,0:T(8,128)S(1)}, f32[8,128]{1,0:T(8,128)S(1)}) custom-call(f32[16,8,8,256]{3,2,1,0:T(8,128)S(1)} %copy-done, f32[8,8,256]{2,1,0:T(8,128)S(1)} %copy-done.1), custom_call_target="tpu_custom_call" | custom-call | tf_op jit(solution)/shard_map/pallas_call | solution.py:568
  82.6 0.6 reshape.7
  83.2 1.0 %copy.5 = f32[16,8,8,256]{3,2,1,0:T(8,128)} copy(f32[16,8,8,256]{3,2,1,0:T(8,128)S(1)} %get-tuple-element.8) | data formatting | bytes 2097152
  (1 shorter events, 0.0 us)
Async XLA Ops:
  0.6 1.2 %copy-start = (f32[16,8,8,256]{3,2,1,0:T(8,128)S(1)}, f32[16,8,8,256]{3,2,1,0:T(8,128)}, u32[]{:S(2)}) copy-start(f32[16,8,8,256]{3,2,1,0:T(8,128)} %refs_0_.1) | copy-start | bytes 3145732
  1.9 0.8 copy-start.1

commit v4 on v3

--- a/solution.py
+++ b/solution.py
@@ -24,7 +24,7 @@
     (
         orb, app, res, cor, rsp, rem, coarse,
         fys, fyr, fzs, fzr, hy, beside, czs, czr, czm, dup, duph, dupz,
-        acc, scal, keep, red, pot, load_sem, send_sem, recv_sem, rsend, rrecv,
+        acc, scal, keep, red, pot, load_sem, send_sem, recv_sem, rsend, rrecv, greet_y, greet_z,
     ) = scratch
     nx, ny, nz = sizes
     bands, xs = orb_hbm.shape[0], orb_hbm.shape[1]
@@ -79,8 +79,23 @@
 
             lax.fori_loop(1, devices, step, 0)
 
+    for level in (0, 2):
+        for turn in range(2):
+            for X in (0, 1 + xc):
+                for g in range(GROUPS):
+                    for t in range(tiles):
+                        beside[turn * COARSE_SWEEPS + level, g, X, t] = jnp.zeros((ROWS, LANES), jnp.float32)
+
+    def greet(semaphore, axes):
+        for k in axes:
+            for d in range(1, sizes[k]):
+                pl.semaphore_signal(semaphore, inc=1, device_id={AXES[k]: wrap(k, d)}, device_id_type=MESH)
+
+    def greeted(semaphore, axes):
+        pl.semaphore_wait(semaphore, sum(sizes[k] - 1 for k in axes))
+
     barrier = pltpu.get_barrier_semaphore()
-    every_peer(lambda to: pl.semaphore_signal(barrier, inc=1, device_id=to, device_id_type=MESH))
+    greet(barrier, (0, 1, 2))
 
     row = lax.broadcasted_iota(jnp.int32, (ROWS, LANES), 0)
     lane = lax.broadcasted_iota(jnp.int32, (ROWS, LANES), 1)
@@ -91,6 +106,8 @@
     first_of_eight = lane % 8 < 4
     top_half = row < ROWS // 2
 
+    z_ends = (right[2], left[2])[: 1 if nz == 2 else 2]
+
     def roll(v, k, axis):
         return pltpu.roll(v, k % v.shape[axis], axis)
 
@@ -107,33 +124,29 @@
 
         lax.fori_loop(lo, hi, step, 0)
 
-    def remote(src, dst, slot, k, axis, target):
+    def remote(src, dst, turn, g, k, to):
         return pltpu.make_async_remote_copy(
             src_ref=src,
             dst_ref=dst,
-            send_sem=send_sem.at[slot, k],
-            recv_sem=recv_sem.at[slot, k],
-            device_id={axis: target},
+            send_sem=send_sem.at[g, k],
+            recv_sem=recv_sem.at[turn % 2, g, k],
+            device_id=to,
             device_id_type=MESH,
         )
 
-    def z_copies(src, dst_l, dst_r, slot):
-        copies = [remote(src, dst_l, slot, 4, "gz", right[2])]
-        if nz > 2:
-            copies.append(remote(src, dst_r, slot, 5, "gz", left[2]))
-        return copies
-
     def fine_copies(field, which, depth, g):
-        slot = which * GROUPS + g
         part = pl.ds(g * per, per)
         ys, yr = fys[which], fyr[which]
         zs, zr = fzs[which], fzr[which]
-        return [
-            remote(field.at[part, pl.ds(2 + xs - depth, depth)], field.at[part, pl.ds(2 - depth, depth)], slot, 0, "gx", right[0]),
-            remote(field.at[part, pl.ds(2, depth)], field.at[part, pl.ds(2 + xs, depth)], slot, 1, "gx", left[0]),
-            remote(ys.at[0, part], yr.at[0, part], slot, 2, "gy", right[1]),
-            remote(ys.at[1, part], yr.at[1, part], slot, 3, "gy", left[1]),
-        ] + z_copies(zs.at[part], zr.at[0, part], zr.at[1, part], slot)
+        moves = [
+            (field.at[part, pl.ds(2 + xs - depth, depth)], field.at[part, pl.ds(2 - depth, depth)], {"gx": right[0]}),
+            (field.at[part, pl.ds(2, depth)], field.at[part, pl.ds(2 + xs, depth)], {"gx": left[0]}),
+            (ys.at[0, part], yr.at[0, part], {"gy": right[1]}),
+            (ys.at[1, part], yr.at[1, part], {"gy": left[1]}),
+        ]
+        for end, z in enumerate(z_ends):
+            moves.append((zs.at[part], zr.at[end, part], {"gz": z}))
+        return [remote(src, dst, which, g, k, to) for k, (src, dst, to) in enumerate(moves)]
 
     def fine_send(field, which, depth, g):
         view = flat(field)
@@ -262,9 +275,9 @@
                 coarse[level, g, 2 + X, t] = jnp.where(even_row, lanes[0], lanes[1])
 
     def coarse_copies(level, w, g):
-        slot = (4 + w) * GROUPS + g
         own, side = coarse.at[level, g], beside.at[level, g]
         low, high = pl.ds(0, ROWS // 2), pl.ds(ROWS // 2, ROWS // 2)
+        top, bottom = pl.ds(0, 2), pl.ds(ROWS - 2, 2)
         inner, last, first = pl.ds(2, xc), 1 + xc, 2
         right_x, left_x = {"gx": right[0]}, {"gx": left[0]}
         right_y, left_y = {"gy": right[1]}, {"gy": left[1]}
@@ -273,25 +286,21 @@
             (own.at[pl.ds(2, 2)], own.at[pl.ds(2 + xc, 2)], left_x),
             (own.at[inner, :, high], side.at[pl.ds(1, xc), :, high], right_y),
             (own.at[inner, :, low], side.at[pl.ds(1, xc), :, low], left_y),
-            (own.at[last, :, high], side.at[0, :, high], right_x | right_y),
-            (own.at[last, :, low], side.at[0, :, low], right_x | left_y),
-            (own.at[first, :, high], side.at[1 + xc, :, high], left_x | right_y),
-            (own.at[first, :, low], side.at[1 + xc, :, low], left_x | left_y),
         ]
-        for end, z in enumerate((right[2], left[2])[: 1 if nz == 2 else 2]):
-            for i, to in enumerate(({}, right_x, left_x, right_y, left_y)):
+        for end, z in enumerate(z_ends):
+            moves.append((czs.at[w, g], czr.at[w, 0, end, g], {"gz": z}))
+        moves += [
+            (own.at[last, :, bottom], side.at[0, :, bottom], right_x | right_y),
+            (own.at[last, :, top], side.at[0, :, top], right_x | left_y),
+            (own.at[first, :, bottom], side.at[1 + xc, :, bottom], left_x | right_y),
+            (own.at[first, :, top], side.at[1 + xc, :, top], left_x | left_y),
+        ]
+        for end, z in enumerate(z_ends):
+            for i, to in ((1, right_x), (2, left_x)):
                 moves.append((czs.at[w, g], czr.at[w, i, end, g], to | {"gz": z}))
-        return [
-            pltpu.make_async_remote_copy(
-                src_ref=src,
-                dst_ref=dst,
-                send_sem=send_sem.at[slot, k],
-                recv_sem=recv_sem.at[slot, k],
-                device_id=to,
-                device_id_type=MESH,
-            )
-            for k, (src, dst, to) in enumerate(moves)
-        ]
+            for part, to in ((bottom, right_y), (top, left_y)):
+                moves.append((czs.at[w, g, part], czr.at[w, 3, end, g, part], to | {"gz": z}))
+        return [remote(src, dst, w, g, k, to) for k, (src, dst, to) in enumerate(moves)]
 
     def coarse_send(level, w, g):
         packed = jnp.zeros((ROWS, LANES), jnp.float32)
@@ -321,8 +330,8 @@
             coarse[level + 1, g, 2 + X, t] = update(vs[t], s, coarse[zero, g, 2 + X, t])
 
     def sweep_wide(zero, level, w, g):
-        zc, from_left, from_right, from_below, from_above = (z_edges(w, i, g) for i in range(5))
-        zs, zy = czs[w, g], jnp.where(top_half, from_above, from_below)
+        zc, from_left, from_right, zy = (z_edges(w, i, g) for i in range(4))
+        zs = czs[w, g]
         for X in range(-1, xc + 1):
             if X < 0:
                 hz = z_halo(from_left, xc - 1)
@@ -529,9 +538,13 @@
         loop(g * per, (g + 1) * per, prepare_second)
         coarse_begin(1, g)
 
-    pl.semaphore_wait(barrier, devices - 1)
+    greeted(barrier, (0, 1, 2))
+    greet(greet_y, (1,))
     loop(0, GROUPS, begin)
+    greeted(greet_y, (1,))
+    greet(greet_z, (2,))
     pot_load.wait()
+    greeted(greet_z, (2,))
     loop(0, GROUPS, first_hamiltonian)
     loop(0, GROUPS, first_residual)
     coarse_solve(0, use_first, lambda g: fine_send(cor, 2, 2, g))
@@ -549,7 +562,7 @@
         tile = (ROWS, LANES)
         vmem = lambda *s: pltpu.VMEM(s + tile, jnp.float32)
         field = vmem(bands, xs + 4, tiles)
-        exchanges = 8
+        moves = 8 + 5 * (1 if sizes[2] == 2 else 2)
         assert bands == QUAD * GROUPS
         devices = sizes[0] * sizes[1] * sizes[2]
         per = bands // GROUPS
@@ -589,7 +602,7 @@
                 vmem(bands, xs, tiles),
                 vmem(2 * COARSE_SWEEPS, GROUPS, xs // 2 + 2, tiles),
                 vmem(4, GROUPS),
-                vmem(4, 5, 2, GROUPS),
+                vmem(4, 4, 2, GROUPS),
                 vmem(4, GROUPS),
                 vmem(QUAD, xs // 2 + 2, tiles),
                 vmem(QUAD, xs // 2, tiles),
@@ -600,13 +613,15 @@
                 pltpu.VMEM((2 * GROUPS, devices, 1, LANES), jnp.float32),
                 pltpu.VMEM(potential.shape, jnp.float32),
                 pltpu.SemaphoreType.DMA((GROUPS + 1, tiles)),
-                pltpu.SemaphoreType.DMA((exchanges * GROUPS, 18)),
-                pltpu.SemaphoreType.DMA((exchanges * GROUPS, 18)),
+                pltpu.SemaphoreType.DMA((GROUPS, moves)),
+                pltpu.SemaphoreType.DMA((2, GROUPS, moves)),
                 pltpu.SemaphoreType.DMA((2 * GROUPS,)),
                 pltpu.SemaphoreType.DMA((2 * GROUPS,)),
+                pltpu.SemaphoreType.REGULAR,
+                pltpu.SemaphoreType.REGULAR,
             ],
             compiler_params=pltpu.CompilerParams(
-                collective_id=0, has_side_effects=True, vmem_limit_bytes=48 * 1024 * 1024
+                collective_id=0, has_side_effects=True, vmem_limit_bytes=53760 * 1024
             ),
         )(orbitals, potential)
         return updated, trial[:GROUPS, :per].reshape(bands)

time: 84.4 us -> 70.8 us (0.84)
  Pallas kernels: 79.9 us -> 67.6 us
  local copies, waits for them, and re-layouts: 3.62 us -> 2.4 us
    pallas_call x1, Pallas kernels: 79.9 us -> 67.6 us  [body(): pl.pallas_call(call, out_shape=(jax.ShapeDtypeStruct(orbitals.shape, jnp....]
    unnamed x5 -> x3, local copies, waits for them, and re-layouts: 3.03 us -> 1.8 us
where the time goes in v4:
time: 70.8 us; the launch traced here: 70.6 us
  Pallas kernels  67.6 us (95%)
  local copies, waits for them, and re-layouts  2.4 us (3%)
    pallas_call x1, Pallas kernels, body(): pl.pallas_call(call, out_shape=(jax.ShapeDtypeStruct(orbitals.shape, jnp....  67.6 us
    unnamed x3, local copies, waits for them, and re-layouts  1.8 us

profile of v4, /device:TPU:0, one launch (start us, length us, event | category | flops | bytes accessed | tf_op | source)
XLA Modules:
  0.0 70.6 jit_solution(2360064429901382893)
XLA Ops:
  0.6 0.0 copy-start
  0.6 0.8 %copy-done = f32[8,8,256]{2,1,0:T(8,128)S(1)} copy-done((f32[8,8,256]{2,1,0:T(8,128)S(1)}, f32[8,8,256]{2,1,0:T(8,128)}, u32[]{:S(2)}) %copy-start) | copy-done | bytes 65560
  1.5 67.6 %shard_map.41 = (f32[16,8,8,256]{3,2,1,0:T(8,128)S(1)}, f32[8,128]{1,0:T(8,128)S(1)}) custom-call(f32[16,8,8,256]{3,2,1,0:T(8,128)} %refs_0_.1, f32[8,8,256]{2,1,0:T(8,128)S(1)} %copy-done), custom_call_target="tpu_custom_call" | custom-call | tf_op jit(solution)/shard_map/pallas_call | solution.py:581
  69.1 0.6 reshape.7
  69.7 1.0 %copy.5 = f32[16,8,8,256]{3,2,1,0:T(8,128)} copy(f32[16,8,8,256]{3,2,1,0:T(8,128)S(1)} %get-tuple-element.8) | data formatting | bytes 2097152
  (1 shorter events, 0.0 us)
Async XLA Ops:
  0.6 0.8 %copy-start = (f32[8,8,256]{2,1,0:T(8,128)S(1)}, f32[8,8,256]{2,1,0:T(8,128)}, u32[]{:S(2)}) copy-start(f32[8,8,256]{2,1,0:T(8,128)} %refs_1_.1) | copy-start | bytes 196612

commit v5 on v4

--- a/solution.py
+++ b/solution.py
@@ -1,4 +1,5 @@
 import functools
+import math
 
 import jax
 import jax.numpy as jnp
@@ -9,6 +10,7 @@
 
 COARSE_SWEEPS = 4
 QUAD = 4
+AHEAD = 2
 WEIGHT = 0.8
 COARSE_DIAG = 1.75
 EPSILON = 1e-06
@@ -24,7 +26,7 @@
     (
         orb, app, res, cor, rsp, rem, coarse,
         fys, fyr, fzs, fzr, hy, beside, czs, czr, czm, dup, duph, dupz,
-        acc, scal, keep, red, pot, load_sem, send_sem, recv_sem, rsend, rrecv, greet_y, greet_z,
+        acc, scal, keep, red, pot, blank, load_sem, send_sem, recv_sem, rsend, rrecv, greet_y, greet_z,
     ) = scratch
     nx, ny, nz = sizes
     bands, xs = orb_hbm.shape[0], orb_hbm.shape[1]
@@ -124,17 +126,23 @@
 
         lax.fori_loop(lo, hi, step, 0)
 
-    def remote(src, dst, turn, g, k, to):
-        return pltpu.make_async_remote_copy(
-            src_ref=src,
-            dst_ref=dst,
-            send_sem=send_sem.at[g, k],
-            recv_sem=recv_sem.at[turn % 2, g, k],
-            device_id=to,
-            device_id_type=MESH,
-        )
-
-    def fine_copies(field, which, depth, g):
+    def send(moves, turn, g):
+        for src, dst, to in moves:
+            pltpu.make_async_remote_copy(
+                src_ref=src,
+                dst_ref=dst,
+                send_sem=send_sem.at[g],
+                recv_sem=recv_sem.at[turn % 2, g],
+                device_id=to,
+                device_id_type=MESH,
+            ).start()
+
+    def arrive(moves, turn, g):
+        part = blank.at[pl.ds(0, sum(math.prod(src.shape) for src, _, _ in moves) // LANES)]
+        pltpu.make_async_copy(part, part, recv_sem.at[turn % 2, g]).wait()
+        pltpu.make_async_copy(part, part, send_sem.at[g]).wait()
+
+    def fine_moves(field, which, depth, g):
         part = pl.ds(g * per, per)
         ys, yr = fys[which], fyr[which]
         zs, zr = fzs[which], fzr[which]
@@ -146,9 +154,9 @@
         ]
         for end, z in enumerate(z_ends):
             moves.append((zs.at[part], zr.at[end, part], {"gz": z}))
-        return [remote(src, dst, which, g, k, to) for k, (src, dst, to) in enumerate(moves)]
-
-    def fine_send(field, which, depth, g):
+        return moves
+
+    def fine_pack(field, which, depth, g):
         view = flat(field)
         span = field.shape[1]
         ys, zs = fys[which], fzs[which]
@@ -165,8 +173,15 @@
                 packed = jnp.where(lane // 4 == x, roll(w, 2 + 4 * x, 1), packed)
             zs[b] = packed
 
-        loop(g * per, (g + 1) * per, pack)
-        start(fine_copies(field, which, depth, g))
+        for k in range(per):
+            pack(g * per + k)
+
+    def fine_send(field, which, depth, g):
+        fine_pack(field, which, depth, g)
+        send(fine_moves(field, which, depth, g), which, g)
+
+    def fine_arrive(field, which, depth, g):
+        arrive(fine_moves(field, which, depth, g), which, g)
 
     def z_packed(zr, b):
         if nz > 2:
@@ -274,7 +289,7 @@
                 lanes = [jnp.where(even_lane, dup[k, 1 + X, t], dup[k + 1, 1 + X, t]) for k in (0, 2)]
                 coarse[level, g, 2 + X, t] = jnp.where(even_row, lanes[0], lanes[1])
 
-    def coarse_copies(level, w, g):
+    def coarse_moves(level, w, g):
         own, side = coarse.at[level, g], beside.at[level, g]
         low, high = pl.ds(0, ROWS // 2), pl.ds(ROWS // 2, ROWS // 2)
         top, bottom = pl.ds(0, 2), pl.ds(ROWS - 2, 2)
@@ -300,7 +315,7 @@
                 moves.append((czs.at[w, g], czr.at[w, i, end, g], to | {"gz": z}))
             for part, to in ((bottom, right_y), (top, left_y)):
                 moves.append((czs.at[w, g, part], czr.at[w, 3, end, g, part], to | {"gz": z}))
-        return [remote(src, dst, w, g, k, to) for k, (src, dst, to) in enumerate(moves)]
+        return moves
 
     def coarse_send(level, w, g):
         packed = jnp.zeros((ROWS, LANES), jnp.float32)
@@ -308,7 +323,7 @@
             v = jnp.where(low_half, coarse[level, g, 2 + X, 0], coarse[level, g, 2 + X, tiles - 1])
             packed = jnp.where(lane // 8 == X, roll(v, 8 * X + 4, 1), packed)
         czs[w, g] = packed
-        start(coarse_copies(level, w, g))
+        send(coarse_moves(level, w, g), w, g)
 
     def z_edges(w, i, g):
         if nz > 2:
@@ -475,13 +490,13 @@
         w = 2 * turn
 
         def middle(g):
-            wait(coarse_copies(zero, w, g))
+            arrive(coarse_moves(zero, w, g), w, g)
             sweep_wide(zero, zero, w, g)
             sweep_own(zero, zero + 1, w, g)
             coarse_send(zero + 2, w + 1, g)
 
         def finish(g):
-            wait(coarse_copies(zero + 2, w + 1, g))
+            arrive(coarse_moves(zero + 2, w + 1, g), w + 1, g)
             sweep_wide(zero, zero + 2, w + 1, g)
             prolong(zero + 3, w + 1, g, use)
             then(g)
@@ -494,7 +509,7 @@
         fine_send(orb, 0, 2, g)
 
     def first_hamiltonian(g):
-        wait(fine_copies(orb, 0, 2, g))
+        fine_arrive(orb, 0, 2, g)
         loop(g * per, (g + 1) * per, functools.partial(apply_one, g))
         reduce_start(0, g, 2)
         fine_send(app, 1, 1, g)
@@ -505,12 +520,12 @@
         for i, v in enumerate((norm_orbitals, first_energy, energy)):
             keep[i, g] = v
         put(0, g, energy)
-        wait(fine_copies(app, 1, 1, g))
+        fine_arrive(app, 1, 1, g)
         loop(g * per, (g + 1) * per, prepare_first)
         coarse_begin(0, g)
 
     def second_hamiltonian(g):
-        wait(fine_copies(cor, 2, 2, g))
+        fine_arrive(cor, 2, 2, g)
         loop(g * per, (g + 1) * per, functools.partial(respond_one, g))
         reduce_start(1, g, NDOTS)
         fine_send(rsp, 3, 1, g)
@@ -534,13 +549,18 @@
         put(2, g, mix * lam)
         put(3, g, mix * change)
         put(4, g, mix * change * lam)
-        wait(fine_copies(rsp, 3, 1, g))
+        fine_arrive(rsp, 3, 1, g)
         loop(g * per, (g + 1) * per, prepare_second)
         coarse_begin(1, g)
 
+    for g in range(AHEAD):
+        wait(load_copies(g))
+        fine_pack(orb, 0, 2, g)
     greeted(barrier, (0, 1, 2))
+    for g in range(AHEAD):
+        send(fine_moves(orb, 0, 2, g), 0, g)
     greet(greet_y, (1,))
-    loop(0, GROUPS, begin)
+    loop(AHEAD, GROUPS, begin)
     greeted(greet_y, (1,))
     greet(greet_z, (2,))
     pot_load.wait()
@@ -562,7 +582,6 @@
         tile = (ROWS, LANES)
         vmem = lambda *s: pltpu.VMEM(s + tile, jnp.float32)
         field = vmem(bands, xs + 4, tiles)
-        moves = 8 + 5 * (1 if sizes[2] == 2 else 2)
         assert bands == QUAD * GROUPS
         devices = sizes[0] * sizes[1] * sizes[2]
         per = bands // GROUPS
@@ -612,9 +631,10 @@
                 vmem(3, GROUPS),
                 pltpu.VMEM((2 * GROUPS, devices, 1, LANES), jnp.float32),
                 pltpu.VMEM(potential.shape, jnp.float32),
+                pltpu.VMEM(((8 * tiles + 2) * ROWS * per, LANES), jnp.float32),
                 pltpu.SemaphoreType.DMA((GROUPS + 1, tiles)),
-                pltpu.SemaphoreType.DMA((GROUPS, moves)),
-                pltpu.SemaphoreType.DMA((2, GROUPS, moves)),
+                pltpu.SemaphoreType.DMA((GROUPS,)),
+                pltpu.SemaphoreType.DMA((2, GROUPS)),
                 pltpu.SemaphoreType.DMA((2 * GROUPS,)),
                 pltpu.SemaphoreType.DMA((2 * GROUPS,)),
                 pltpu.SemaphoreType.REGULAR,

time: 70.8 us -> 69 us (0.975)
  Pallas kernels: 67.6 us -> 65.8 us
    pallas_call x1, Pallas kernels: 67.6 us -> 65.8 us  [body(): pl.pallas_call(call, out_shape=(jax.ShapeDtypeStruct(orbitals.shape, jnp....]
where the time goes in v5:
time: 69 us; the launch traced here: 68.8 us
  Pallas kernels  65.8 us (95%)
  local copies, waits for them, and re-layouts  2.4 us (3%)
    pallas_call x1, Pallas kernels, body(): pl.pallas_call(call, out_shape=(jax.ShapeDtypeStruct(orbitals.shape, jnp....  65.8 us
    unnamed x3, local copies, waits for them, and re-layouts  1.8 us

profile of v5, /device:TPU:0, one launch (start us, length us, event | category | flops | bytes accessed | tf_op | source)
XLA Modules:
  0.0 68.8 jit_solution(5450986044726639818)
XLA Ops:
  0.6 0.0 copy-start
  0.6 0.8 %copy-done = f32[8,8,256]{2,1,0:T(8,128)S(1)} copy-done((f32[8,8,256]{2,1,0:T(8,128)S(1)}, f32[8,8,256]{2,1,0:T(8,128)}, u32[]{:S(2)}) %copy-start) | copy-done | bytes 65560
  1.5 65.8 %shard_map.41 = (f32[16,8,8,256]{3,2,1,0:T(8,128)S(1)}, f32[8,128]{1,0:T(8,128)S(1)}) custom-call(f32[16,8,8,256]{3,2,1,0:T(8,128)} %refs_0_.1, f32[8,8,256]{2,1,0:T(8,128)S(1)} %copy-done), custom_call_target="tpu_custom_call" | custom-call | tf_op jit(solution)/shard_map/pallas_call | solution.py:600
  67.3 0.6 reshape.7
  67.9 1.0 %copy.5 = f32[16,8,8,256]{3,2,1,0:T(8,128)} copy(f32[16,8,8,256]{3,2,1,0:T(8,128)S(1)} %get-tuple-element.8) | data formatting | bytes 2097152
  (1 shorter events, 0.0 us)
Async XLA Ops:
  0.6 0.8 %copy-start = (f32[8,8,256]{2,1,0:T(8,128)S(1)}, f32[8,8,256]{2,1,0:T(8,128)}, u32[]{:S(2)}) copy-start(f32[8,8,256]{2,1,0:T(8,128)} %refs_1_.1) | copy-start | bytes 196612

commit v6 on v5

--- a/solution.py
+++ b/solution.py
@@ -11,6 +11,17 @@
 COARSE_SWEEPS = 4
 QUAD = 4
 AHEAD = 2
+ENTRY = "b2"
+ORDER = (
+    "h0 b3 h1 h2",
+    "r0 h3 r1 r2",
+    "m0 r3 m1 m2",
+    "f0 m3 f1 f2 f3",
+    "H0 H1 H2 H3",
+    "R0 R1 R2 R3",
+    "M0 M1 M2 M3",
+    "F0 F1 F2 F3",
+)
 WEIGHT = 0.8
 COARSE_DIAG = 1.75
 EPSILON = 1e-06
@@ -147,10 +158,10 @@
         ys, yr = fys[which], fyr[which]
         zs, zr = fzs[which], fzr[which]
         moves = [
+            (ys.at[0, part], yr.at[0, part], {"gy": right[1]}),
+            (ys.at[1, part], yr.at[1, part], {"gy": left[1]}),
             (field.at[part, pl.ds(2 + xs - depth, depth)], field.at[part, pl.ds(2 - depth, depth)], {"gx": right[0]}),
             (field.at[part, pl.ds(2, depth)], field.at[part, pl.ds(2 + xs, depth)], {"gx": left[0]}),
-            (ys.at[0, part], yr.at[0, part], {"gy": right[1]}),
-            (ys.at[1, part], yr.at[1, part], {"gy": left[1]}),
         ]
         for end, z in enumerate(z_ends):
             moves.append((zs.at[part], zr.at[end, part], {"gz": z}))
@@ -297,24 +308,22 @@
         right_x, left_x = {"gx": right[0]}, {"gx": left[0]}
         right_y, left_y = {"gy": right[1]}, {"gy": left[1]}
         moves = [
-            (own.at[pl.ds(xc, 2)], own.at[pl.ds(0, 2)], right_x),
-            (own.at[pl.ds(2, 2)], own.at[pl.ds(2 + xc, 2)], left_x),
             (own.at[inner, :, high], side.at[pl.ds(1, xc), :, high], right_y),
             (own.at[inner, :, low], side.at[pl.ds(1, xc), :, low], left_y),
-        ]
-        for end, z in enumerate(z_ends):
-            moves.append((czs.at[w, g], czr.at[w, 0, end, g], {"gz": z}))
-        moves += [
             (own.at[last, :, bottom], side.at[0, :, bottom], right_x | right_y),
             (own.at[last, :, top], side.at[0, :, top], right_x | left_y),
             (own.at[first, :, bottom], side.at[1 + xc, :, bottom], left_x | right_y),
             (own.at[first, :, top], side.at[1 + xc, :, top], left_x | left_y),
         ]
         for end, z in enumerate(z_ends):
-            for i, to in ((1, right_x), (2, left_x)):
-                moves.append((czs.at[w, g], czr.at[w, i, end, g], to | {"gz": z}))
             for part, to in ((bottom, right_y), (top, left_y)):
                 moves.append((czs.at[w, g, part], czr.at[w, 3, end, g, part], to | {"gz": z}))
+            for i, to in ((1, right_x), (2, left_x), (0, {})):
+                moves.append((czs.at[w, g], czr.at[w, i, end, g], to | {"gz": z}))
+        moves += [
+            (own.at[pl.ds(xc, 2)], own.at[pl.ds(0, 2)], right_x),
+            (own.at[pl.ds(2, 2)], own.at[pl.ds(2 + xc, 2)], left_x),
+        ]
         return moves
 
     def coarse_send(level, w, g):
@@ -485,24 +494,20 @@
         coarse_pack(turn * COARSE_SWEEPS, g)
         coarse_send(turn * COARSE_SWEEPS, 2 * turn, g)
 
-    def coarse_solve(turn, use, then):
-        zero = turn * COARSE_SWEEPS
-        w = 2 * turn
-
-        def middle(g):
-            arrive(coarse_moves(zero, w, g), w, g)
-            sweep_wide(zero, zero, w, g)
-            sweep_own(zero, zero + 1, w, g)
-            coarse_send(zero + 2, w + 1, g)
-
-        def finish(g):
-            arrive(coarse_moves(zero + 2, w + 1, g), w + 1, g)
-            sweep_wide(zero, zero + 2, w + 1, g)
-            prolong(zero + 3, w + 1, g, use)
-            then(g)
-
-        loop(0, GROUPS, middle)
-        loop(0, GROUPS, finish)
+    def middle(turn, g):
+        zero, w = turn * COARSE_SWEEPS, 2 * turn
+        arrive(coarse_moves(zero, w, g), w, g)
+        sweep_wide(zero, zero, w, g)
+        sweep_own(zero, zero + 1, w, g)
+        coarse_send(zero + 2, w + 1, g)
+
+    def finish(turn, use, g):
+        zero, w = turn * COARSE_SWEEPS, 2 * turn + 1
+        arrive(coarse_moves(zero + 2, w, g), w, g)
+        sweep_wide(zero, zero + 2, w, g)
+        prolong(zero + 3, w, g, use)
+        if turn == 0:
+            fine_send(cor, 2, 2, g)
 
     def begin(g):
         wait(load_copies(g))
@@ -560,17 +565,35 @@
     for g in range(AHEAD):
         send(fine_moves(orb, 0, 2, g), 0, g)
     greet(greet_y, (1,))
-    loop(AHEAD, GROUPS, begin)
+    stages = dict(
+        b=begin,
+        h=first_hamiltonian,
+        r=first_residual,
+        m=functools.partial(middle, 0),
+        f=functools.partial(finish, 0, use_first),
+        H=second_hamiltonian,
+        R=second_residual,
+        M=functools.partial(middle, 1),
+        F=functools.partial(finish, 1, use_second),
+    )
+
+    def run(steps):
+        steps = steps.split()
+        while steps:
+            name, lo = steps[0][0], int(steps[0][1])
+            n = 1
+            while n < len(steps) and steps[n] == f"{name}{lo + n}":
+                n += 1
+            loop(lo, lo + n, stages[name])
+            steps = steps[n:]
+
+    run(ENTRY)
     greeted(greet_y, (1,))
     greet(greet_z, (2,))
     pot_load.wait()
     greeted(greet_z, (2,))
-    loop(0, GROUPS, first_hamiltonian)
-    loop(0, GROUPS, first_residual)
-    coarse_solve(0, use_first, lambda g: fine_send(cor, 2, 2, g))
-    loop(0, GROUPS, second_hamiltonian)
-    loop(0, GROUPS, second_residual)
-    coarse_solve(1, use_second, lambda g: None)
+    for steps in ORDER:
+        run(steps)
 
 
 def solution(mesh):

time: 69 us -> 68.2 us (0.988)
  Pallas kernels: 65.8 us -> 65 us
    pallas_call x1, Pallas kernels: 65.8 us -> 65 us  [body(): pl.pallas_call(call, out_shape=(jax.ShapeDtypeStruct(orbitals.shape, jnp....]
where the time goes in v6:
time: 68.2 us; the launch traced here: 68 us
  Pallas kernels  65 us (95%)
  local copies, waits for them, and re-layouts  2.4 us (4%)
    pallas_call x1, Pallas kernels, body(): pl.pallas_call(call, out_shape=(jax.ShapeDtypeStruct(orbitals.shape, jnp....  65 us
    unnamed x3, local copies, waits for them, and re-layouts  1.8 us

profile of v6, /device:TPU:0, one launch (start us, length us, event | category | flops | bytes accessed | tf_op | source)
XLA Modules:
  0.0 68.0 jit_solution(16661811637208950021)
XLA Ops:
  0.6 0.0 copy-start
  0.6 0.8 %copy-done = f32[8,8,256]{2,1,0:T(8,128)S(1)} copy-done((f32[8,8,256]{2,1,0:T(8,128)S(1)}, f32[8,8,256]{2,1,0:T(8,128)}, u32[]{:S(2)}) %copy-start) | copy-done | bytes 65560
  1.5 65.0 %shard_map.41 = (f32[16,8,8,256]{3,2,1,0:T(8,128)S(1)}, f32[8,128]{1,0:T(8,128)S(1)}) custom-call(f32[16,8,8,256]{3,2,1,0:T(8,128)} %refs_0_.1, f32[8,8,256]{2,1,0:T(8,128)S(1)} %copy-done), custom_call_target="tpu_custom_call" | custom-call | tf_op jit(solution)/shard_map/pallas_call | solution.py:623
  66.5 0.6 reshape.7
  67.1 1.0 %copy.5 = f32[16,8,8,256]{3,2,1,0:T(8,128)} copy(f32[16,8,8,256]{3,2,1,0:T(8,128)S(1)} %get-tuple-element.8) | data formatting | bytes 2097152
  (1 shorter events, 0.0 us)
Async XLA Ops:
  0.6 0.8 %copy-start = (f32[8,8,256]{2,1,0:T(8,128)S(1)}, f32[8,8,256]{2,1,0:T(8,128)}, u32[]{:S(2)}) copy-start(f32[8,8,256]{2,1,0:T(8,128)} %refs_1_.1) | copy-start | bytes 196612

commit v7 on v6

--- a/solution.py
+++ b/solution.py
@@ -544,7 +544,7 @@
             first_energy + lam * ((po + energy * oc) + (rc + energy * oc)) + lam * lam * (pc + energy * cc)
         )
         trial = trial_sum / (trial_norm + EPSILON)
-        energies[pl.ds(g, 1), :] = trial[0:1]
+        keep[3, g] = trial
         change = trial - energy
         projected = lam * rp - change * (ro + lam * rc)
         cross = po + lam * pc
@@ -594,6 +594,10 @@
     greeted(greet_z, (2,))
     for steps in ORDER:
         run(steps)
+    trial = keep[3, 0]
+    for g in range(1, GROUPS):
+        trial = jnp.where(lane // per == g, roll(keep[3, g], g * per, 1), trial)
+    energies[...] = trial[0, :bands]
 
 
 def solution(mesh):
@@ -624,7 +628,7 @@
             call,
             out_shape=(
                 jax.ShapeDtypeStruct(orbitals.shape, jnp.float32),
-                jax.ShapeDtypeStruct(tile, jnp.float32),
+                jax.ShapeDtypeStruct((bands,), jnp.float32),
             ),
             in_specs=[
                 pl.BlockSpec(memory_space=pltpu.HBM),
@@ -651,7 +655,7 @@
                 vmem(QUAD, xs // 2),
                 pltpu.VMEM((2, GROUPS, NDOTS * per, LANES), jnp.float32),
                 pltpu.VMEM((5, bands, LANES), jnp.float32),
-                vmem(3, GROUPS),
+                vmem(4, GROUPS),
                 pltpu.VMEM((2 * GROUPS, devices, 1, LANES), jnp.float32),
                 pltpu.VMEM(potential.shape, jnp.float32),
                 pltpu.VMEM(((8 * tiles + 2) * ROWS * per, LANES), jnp.float32),
@@ -667,7 +671,7 @@
                 collective_id=0, has_side_effects=True, vmem_limit_bytes=53760 * 1024
             ),
         )(orbitals, potential)
-        return updated, trial[:GROUPS, :per].reshape(bands)
+        return updated, trial
 
     return jax.shard_map(
         body,

time: 68.2 us -> 68.2 us (level)
    unnamed x3 -> x4, local copies, waits for them, and re-layouts: 1.8 us -> 2.32 us
where the time goes in v7:
time: 68.2 us; the launch traced here: 68 us
  Pallas kernels  65.1 us (95%)
  local copies, waits for them, and re-layouts  2.32 us (3%)
    pallas_call x1, Pallas kernels, body(): pl.pallas_call(call, out_shape=(jax.ShapeDtypeStruct(orbitals.shape, jnp....  65.1 us
    unnamed x4, local copies, waits for them, and re-layouts  2.32 us

profile of v7, /device:TPU:0, one launch (start us, length us, event | category | flops | bytes accessed | tf_op | source)
XLA Modules:
  0.0 68.0 jit_solution(14092419702801737849)
XLA Ops:
  0.6 0.0 copy-start
  0.6 0.8 %copy-done = f32[8,8,256]{2,1,0:T(8,128)S(1)} copy-done((f32[8,8,256]{2,1,0:T(8,128)S(1)}, f32[8,8,256]{2,1,0:T(8,128)}, u32[]{:S(2)}) %copy-start) | copy-done | bytes 65560
  1.5 65.1 %shard_map.41 = (f32[16,8,8,256]{3,2,1,0:T(8,128)S(1)}, f32[16]{0:T(128)S(1)}) custom-call(f32[16,8,8,256]{3,2,1,0:T(8,128)} %refs_0_.1, f32[8,8,256]{2,1,0:T(8,128)S(1)} %copy-done), custom_call_target="tpu_custom_call" | custom-call | tf_op jit(solution)/shard_map/pallas_call | solution.py:627
  66.5 1.0 %copy.6 = f32[16,8,8,256]{3,2,1,0:T(8,128)} copy(f32[16,8,8,256]{3,2,1,0:T(8,128)S(1)} %get-tuple-element.4) | data formatting | bytes 2097152
  67.5 0.5 copy.7
Async XLA Ops:
  0.6 0.8 %copy-start = (f32[8,8,256]{2,1,0:T(8,128)S(1)}, f32[8,8,256]{2,1,0:T(8,128)}, u32[]{:S(2)}) copy-start(f32[8,8,256]{2,1,0:T(8,128)} %refs_1_.1) | copy-start | bytes 196612
